TPU v7x, 256 devices: a whole 4x4x8 slice. The times are simulated.
256 devices in a mesh: seq: 32 (over y, x, core), head: 8 (over z).
Axes of the slice: x: 4, y: 4, z: 8, core: 2. Of those that a mesh axis runs over, the one named last changes fastest.
Arguments:
- patch_embed: bfloat16 [32, 1024, 1280], P('head', 'seq'), may hold values from -6 to 6
- perturbation: float32 [32, 1024, 1280], P('head', 'seq'), may hold values from -3 to 3
- target: bfloat16 [32, 1024, 1280], P('head', 'seq'), may hold values from -6 to 6
- ln_gain: float32 [1280], replicated, may hold values from 0.5 to 1.5
- ln_bias: float32 [1280], replicated, may hold values from -1.5 to 1.5
- w_qkv: bfloat16 [16, 240, 1280], P('head'), may hold values from -10.0623059 to 10.0623059
- w_out: bfloat16 [16, 80, 1280], P('head'), may hold values from -0.15625 to 0.15625
- radius: float32 [32], replicated, may hold values from 137.38402 to 423.6007
- step_size: float32 [32], replicated, may hold values from 34.346004 to 137.38402
Outputs:
- perturbation_out: float32 [32, 1024, 1280], P('head', 'seq')
All inputs are finite; a program needn't handle non-finite values.
Results may differ from a plain program's by a relative error of at most 0.001.
Values may be sent and summed in bfloat16 or wider, within the bound.
A program may use at most 64 MiB of HBM per device.

v0:
```python
import math

import jax
import jax.numpy as jnp
from jax import lax
from jax.sharding import PartitionSpec as P

norm_epsilon = 1e-06
layer_epsilon = 1e-06


def copy_for_each(value, axis):
    copies = jnp.broadcast_to(value, (lax.axis_size(axis), *value.shape))
    return lax.all_to_all(copies, axis, split_axis=0, concat_axis=0, tiled=True)


def over_copies(value, axis):
    everything = copy_for_each(value, axis)
    return jnp.sum(everything, axis=0)


def in_one(arrays, axis):
    ends = [0]
    for a in arrays:
        ends.append(ends[-1] + a.size)
    so_far = over_copies(jnp.concatenate([a.ravel() for a in arrays]), axis)
    return tuple((so_far[b:e].reshape(a.shape) for a, b, e in zip(arrays, ends, ends[1:])))


def layer_statistics(gathered):
    center = gathered - jnp.mean(gathered, axis=-1, keepdims=True)
    variance = jnp.mean(center * center, axis=-1, keepdims=True)
    inverse = lax.rsqrt(variance + layer_epsilon)
    return (center * inverse, inverse)


def attend_forward(queries, key_rows, values, score_scale):
    item_count, length, head_dim = queries.shape
    block_rows = min(512, length)
    query_blocks = queries.reshape(item_count, length // block_rows, block_rows, head_dim).swapaxes(
        0, 1
    )

    def one_block(query_block):
        scores = (
            jnp.einsum("nqe,nke->nqk", query_block, key_rows, preferred_element_type=jnp.float32)
            * score_scale
        )
        row_max = jnp.max(scores, axis=-1, keepdims=True)
        log_total = row_max + jnp.log(jnp.sum(jnp.exp(scores - row_max), axis=-1, keepdims=True))
        weights = jnp.exp(scores - log_total).astype(jnp.bfloat16)
        output = jnp.einsum(
            "nqk,nke->nqe", weights, values, preferred_element_type=jnp.float32
        ).astype(jnp.bfloat16)
        return (output, log_total[..., 0])

    output, log_total = lax.map(one_block, query_blocks)
    output = output.swapaxes(0, 1).reshape(item_count, length, head_dim)
    log_total = log_total.swapaxes(0, 1).reshape(item_count, length)
    return (output, log_total)


def attend_backward(queries, key_rows, values, output, log_total, grad_output, score_scale):
    item_count, length, head_dim = queries.shape
    block_rows = min(512, length)
    block_count = length // block_rows

    def cut_rows(array):
        return array.reshape((item_count, block_count, block_rows) + array.shape[2:]).swapaxes(0, 1)

    row_dot = jnp.sum(grad_output.astype(jnp.float32) * output.astype(jnp.float32), axis=-1)

    def one_block(carry, inputs):
        grad_keys, grad_values = carry
        query_block, grad_block, total_block, dot_block = inputs
        scores = (
            jnp.einsum("nqe,nke->nqk", query_block, key_rows, preferred_element_type=jnp.float32)
            * score_scale
        )
        weights = jnp.exp(scores - total_block[..., None])
        grad_values = grad_values + jnp.einsum(
            "nqk,nqe->nke",
            weights.astype(jnp.bfloat16),
            grad_block,
            preferred_element_type=jnp.float32,
        )
        grad_weights = jnp.einsum(
            "nqe,nke->nqk", grad_block, values, preferred_element_type=jnp.float32
        )
        grad_scores = (weights * (grad_weights - dot_block[..., None]) * score_scale).astype(
            jnp.bfloat16
        )
        grad_query = jnp.einsum(
            "nqk,nke->nqe", grad_scores, key_rows, preferred_element_type=jnp.float32
        ).astype(jnp.bfloat16)
        grad_keys = grad_keys + jnp.einsum(
            "nqk,nqe->nke", grad_scores, query_block, preferred_element_type=jnp.float32
        )
        return ((grad_keys, grad_values), grad_query)

    zero_rows = jnp.zeros((item_count, length, head_dim), jnp.float32)
    (grad_keys, grad_values), grad_query = lax.scan(
        one_block,
        (zero_rows, zero_rows),
        (cut_rows(queries), cut_rows(grad_output), cut_rows(log_total), cut_rows(row_dot)),
    )
    grad_query = grad_query.swapaxes(0, 1).reshape(item_count, length, head_dim)
    return jnp.concatenate(
        [grad_query, grad_keys.astype(jnp.bfloat16), grad_values.astype(jnp.bfloat16)], axis=-1
    )


def on_device(patch_embed, perturbation, target, ln_gain, ln_bias, w_qkv, w_out, radius, step_size):
    own_images, part_rows, model_width = patch_embed.shape
    head_dim = w_qkv.shape[1] // 3
    first_image = lax.axis_index("head") * own_images
    own_step = lax.dynamic_slice_in_dim(step_size, first_image, own_images, 0)
    own_radius = lax.dynamic_slice_in_dim(radius, first_image, own_images, 0)
    score_scale = 1.0 / math.sqrt(head_dim)
    qkv_every, out_every = (
        lax.all_gather(w_qkv, "head", axis=0, tiled=True),
        lax.all_gather(w_out, "head", axis=0, tiled=True),
    )
    current = perturbation
    mixed = patch_embed.astype(jnp.float32) + current
    rounded = mixed.astype(jnp.bfloat16)
    normed, inverse = layer_statistics(rounded.astype(jnp.float32))
    hidden = (normed * ln_gain + ln_bias).astype(jnp.bfloat16)
    packed_own = jnp.einsum(
        "epd,hcd->ehpc", hidden, qkv_every, preferred_element_type=jnp.float32
    ).astype(jnp.bfloat16)
    packed = lax.all_to_all(packed_own, "head", split_axis=1, concat_axis=0, tiled=True)
    pair_rows = lax.all_to_all(packed, "seq", split_axis=0, concat_axis=2, tiled=True)[0]
    queries = pair_rows[..., :head_dim]
    key_rows = pair_rows[..., head_dim : 2 * head_dim]
    values = pair_rows[..., 2 * head_dim :]
    output, log_total = attend_forward(queries, key_rows, values, score_scale)
    returned = lax.all_to_all(output[None], "seq", split_axis=2, concat_axis=0, tiled=True)
    own_outputs = lax.all_to_all(returned, "head", split_axis=0, concat_axis=1, tiled=True)
    branch = jnp.einsum("ehpc,hcd->epd", own_outputs, out_every, preferred_element_type=jnp.float32)
    result = mixed + branch
    residual = result - target.astype(jnp.float32)
    grad_own = jnp.einsum(
        "epd,hcd->ehpc",
        residual.astype(jnp.bfloat16),
        out_every,
        preferred_element_type=jnp.float32,
    ).astype(jnp.bfloat16)
    grad_output = lax.all_to_all(grad_own, "head", split_axis=1, concat_axis=0, tiled=True)
    grad_pairs = lax.all_to_all(grad_output, "seq", split_axis=0, concat_axis=2, tiled=True)[0]
    grad_packed = attend_backward(
        queries, key_rows, values, output, log_total, grad_pairs, score_scale
    )
    grad_tokens = lax.all_to_all(grad_packed[None], "seq", split_axis=2, concat_axis=0, tiled=True)
    grad_mine = lax.all_to_all(grad_tokens, "head", split_axis=0, concat_axis=1, tiled=True)
    grad_hidden = jnp.einsum(
        "ehpc,hcd->epd", grad_mine, qkv_every, preferred_element_type=jnp.float32
    )
    scaled = grad_hidden * ln_gain
    first_mean = jnp.mean(scaled, axis=-1, keepdims=True)
    second_mean = jnp.mean(scaled * normed, axis=-1, keepdims=True)
    grad_input = (scaled - first_mean - normed * second_mean) * inverse
    gradient = residual + grad_input
    grad_square, cross_sum, own_sum = in_one(
        (
            jnp.sum(gradient * gradient, axis=(1, 2)),
            jnp.sum(current * gradient, axis=(1, 2)),
            jnp.sum(current * current, axis=(1, 2)),
        ),
        "seq",
    )
    factor = own_step / jnp.sqrt(grad_square + norm_epsilon)
    stepped = current + factor[:, None, None] * gradient
    stepped_square = own_sum + 2.0 * factor * cross_sum + factor * factor * grad_square
    current = (
        stepped
        * jnp.minimum(1.0, own_radius / jnp.sqrt(stepped_square + norm_epsilon))[:, None, None]
    )
    return current


def solution(mesh):
    placed = (
        P("head", "seq", None),
        P("head", "seq", None),
        P("head", "seq", None),
        P(),
        P(),
        P("head", None, None),
        P("head", None, None),
        P(),
        P(),
    )
    return jax.shard_map(
        on_device, mesh=mesh, in_specs=placed, out_specs=P("head", "seq", None), check_vma=False
    )
```

profile of v0, /device:TPU:1, one launch (start us, length us, event | category | flops | bytes accessed | tf_op | source)
XLA Modules:
  0.0 377.7 jit_solution(3460362058122214073)
XLA Ops:
  6.5 0.7 all-gather.3.cloned.1.call-update
  7.3 1.3 convert_reduce_fusion
  8.6 0.2 fusion.82
  8.8 111.5 %all-gather.3.cloned.1.call-done = bf16[16,240,1280]{2,1,0:T(8,128)(2,1)} async-done(((bf16[2,240,1280]{2,1,0:T(8,128)(2,1)}), bf16[16,240,1280]{2,1,0:T(8,128)(2,1)}) %all-gather.3.cloned.1.call-update) | async-done | bytes 9830416 | tf_op jit(solution)/shard_map/all_gather | solution.py:121
  120.4 7.1 %fusion.61 = bf16[4,16,32,240]{3,2,1,0:T(8,128)(2,1)S(1)} fusion(bf16[16,240,1280]{2,1,0:T(8,128)(2,1)} %all-gather.3.cloned.1.call-done, bf16[4,32,1280]{2,1,0:T(8,128)(2,1)S(1)} %get-tuple-element.285, f32[1280]{0:T(1024)} %param.17, f32[1280]{0:T(1024)} %param.16, f32[4,32]{1,0:T(4,128)S(1)} %add_rsqrt_fusion, f32[4,32]{1,0:T(4,128)S(1)} %broadcast_multiply_fusion.2), kind=kOutput, calls=%fused_computation.58 | convolution fusion | flops 1259765760 | bytes 11152384 | tf_op jit(solution)/shard_map/epd,hcd->ehpc/dot_general | solution.py:129
  127.5 1.1 copy.161
  128.6 4.1 %all-to-all-start = ((bf16[4,16,32,240]{3,2,0,1:T(8,128)(2,1)}), bf16[4,16,32,240]{3,2,0,1:T(8,128)(2,1)S(1)}, u32[]{:S(2)}, u32[]{:S(2)}) async-start(bf16[4,16,32,240]{3,2,0,1:T(8,128)(2,1)} %copy.161), calls=%async_computation | async-start | bytes 2097152 | tf_op jit(solution)/shard_map/all_to_all | solution.py:132
  132.7 0.7 all-gather.5.cloned.1.call-update
  133.4 32.5 %all-to-all-done = bf16[4,16,32,240]{3,2,0,1:T(8,128)(2,1)S(1)} async-done(((bf16[4,16,32,240]{3,2,0,1:T(8,128)(2,1)}), bf16[4,16,32,240]{3,2,0,1:T(8,128)(2,1)S(1)}, u32[]{:S(2)}, u32[]{:S(2)}) %all-to-all-start) | async-done | bytes 983072 | tf_op jit(solution)/shard_map/all_to_all | solution.py:132
  165.8 1.1 copy.163
  166.9 7.6 %all-to-all-start.1 = ((bf16[32,2,32,240]{3,2,1,0:T(8,128)(2,1)}), bf16[32,2,32,240]{3,2,1,0:T(8,128)(2,1)S(1)}, u32[]{:S(2)}, u32[]{:S(2)}) async-start(bf16[32,2,32,240]{3,2,1,0:T(8,128)(2,1)} %bitcast.10), calls=%async_computation.1 | async-start | bytes 2097152 | tf_op jit(solution)/shard_map/all_to_all | solution.py:133
  174.5 17.0 %all-to-all-done.1 = bf16[32,2,32,240]{3,2,1,0:T(8,128)(2,1)S(1)} async-done(((bf16[32,2,32,240]{3,2,1,0:T(8,128)(2,1)}), bf16[32,2,32,240]{3,2,1,0:T(8,128)(2,1)S(1)}, u32[]{:S(2)}, u32[]{:S(2)}) %all-to-all-start.1) | async-done | bytes 983072 | tf_op jit(solution)/shard_map/all_to_all | solution.py:133
  191.6 0.4 fusion.95
  192.0 0.2 copy.165
  192.2 0.2 copy.166
  192.5 0.2 copy.167
  192.7 5.5 %while.27 = (s32[]{:T(128)}, bf16[2,2,512,80]{2,3,1,0:T(8,128)(2,1)S(1)}, f32[2,2,512]{2,1,0:T(2,128)S(1)}, bf16[2,2,512,80]{2,3,1,0:T(8,128)(2,1)S(1)}, bf16[2,...) while((s32[]{:T(128)}, bf16[2,2,512,80]{2,3,1,0:T(8,128)(2,1)S(1)}, ...), condition=%wide.region_5.6_spmd, body=%wide.region_2.5_spmd.sunk | while | flops 344013824 | bytes 13598809 | solution.py:57
  192.7 0.8 multiply_reduce_fusion.5
  193.6 0.9 exponential_reduce_fusion.2
  194.5 0.9 fusion.124
  195.5 0.8 multiply_reduce_fusion.5
  196.3 0.9 exponential_reduce_fusion.2
  197.3 0.9 fusion.124
  198.3 0.4 copy.196
  198.7 15.0 %all_to_all.144 = bf16[1,2,1024,80]{3,1,0,2:T(2,128)(2,1)S(1)} all-to-all(bf16[1,2,1024,80]{3,1,0,2:T(2,128)(2,1)S(1)} %bitcast.192), channel_id=1, replica_groups=mesh['seq'=32,'head'=8] {'seq'}, dimensions={2} | all-to-all | bytes 655360 | tf_op jit(solution)/shard_map/all_to_all | solution.py:138
  213.9 19.2 %all_to_all.145 = bf16[32,2,32,80]{3,2,1,0:T(8,128)(2,1)S(1)} all-to-all(bf16[32,2,32,80]{3,2,1,0:T(8,128)(2,1)S(1)} %copy.172), channel_id=1, replica_groups=mesh['seq'=32,'head'=8] {'head'}, dimensions={0} | all-to-all | bytes 655360 | tf_op jit(solution)/shard_map/all_to_all | solution.py:139
  233.2 2.8 fusion.55
  236.1 0.1 copy-done.6
  236.2 1.5 fusion.67
  237.8 17.7 %all_to_all.146 = bf16[4,16,32,80]{3,2,0,1:T(8,128)(2,1)S(1)} all-to-all(bf16[4,16,32,80]{3,2,0,1:T(8,128)(2,1)S(1)} %copy.174), channel_id=1, replica_groups=mesh['seq'=32,'head'=8] {'head'}, dimensions={1} | all-to-all | bytes 655360 | tf_op jit(solution)/shard_map/all_to_all | solution.py:149
  255.4 0.8 copy.176
  256.3 8.1 %all-to-all-start.5 = ((bf16[32,2,32,80]{3,2,1,0:T(8,128)(2,1)}), bf16[32,2,32,80]{3,2,1,0:T(8,128)(2,1)S(1)}, u32[]{:S(2)}, u32[]{:S(2)}) async-start(bf16[32,2,32,80]{3,2,1,0:T(8,128)(2,1)} %bitcast.34), calls=%async_computation.5 | async-start | bytes 1048576 | tf_op jit(solution)/shard_map/all_to_all | solution.py:150
  264.4 0.3 copy.168
  264.7 11.1 %all-to-all-done.5 = bf16[32,2,32,80]{3,2,1,0:T(8,128)(2,1)S(1)} async-done(((bf16[32,2,32,80]{3,2,1,0:T(8,128)(2,1)}), bf16[32,2,32,80]{3,2,1,0:T(8,128)(2,1)S(1)}, u32[]{:S(2)}, u32[]{:S(2)}) %all-to-all-start.5) | async-done | bytes 327712 | tf_op jit(solution)/shard_map/all_to_all | solution.py:150
  275.9 0.4 fusion.70
  276.4 0.9 copy.181
  277.3 0.8 broadcast.58
  278.1 18.0 %while.28 = (s32[]{:T(128)}, f32[2,1024,80]{1,2,0:T(8,128)S(1)}, f32[2,1024,80]{1,2,0:T(8,128)}, bf16[2,2,512,80]{2,3,1,0:T(8,128)(2,1)}, bf16[2,2,512,80]{2,3,1...) while((s32[]{:T(128)}, f32[2,1024,80]{1,2,0:T(8,128)S(1)}, ...), condition=%wide.region_8.9_spmd.clone, body=%wide.region_7.8_spmd.clone.sunk | while | flops 849035264 | bytes 60822308 | solution.py:102
  278.1 0.8 fusion.135
  278.9 2.1 copy-done
  281.0 1.5 multiply_convert_fusion.2
  282.5 0.6 convolution_add_fusion.2
  283.1 1.4 fusion.137
  284.6 0.2 copy-done.1
  284.8 1.8 fusion.136
  286.6 0.7 fusion.135
  287.3 2.1 copy-done
  289.4 1.5 multiply_convert_fusion.2
  291.0 0.6 convolution_add_fusion.2
  291.6 1.4 fusion.137
  293.0 0.2 copy-done.1
  293.2 2.9 fusion.136
  296.1 1.0 copy.204
  297.1 1.1 convert_element_type.82
  298.3 0.9 copy.185
  299.3 20.7 %all_to_all.147 = bf16[1,2,1024,240]{3,1,0,2:T(2,128)(2,1)S(1)} all-to-all(bf16[1,2,1024,240]{3,1,0,2:T(2,128)(2,1)S(1)} %copy.185), channel_id=1, replica_groups=mesh['seq'=32,'head'=8] {'seq'}, dimensions={2} | all-to-all | bytes 1966080 | tf_op jit(solution)/shard_map/all_to_all | solution.py:154
  320.0 0.1 copy.186
  320.2 31.6 %all_to_all.148 = bf16[32,2,32,240]{3,2,1,0:T(8,128)(2,1)S(1)} all-to-all(bf16[32,2,32,240]{3,2,1,0:T(8,128)(2,1)S(1)} %copy.187), channel_id=1, replica_groups=mesh['seq'=32,'head'=8] {'head'}, dimensions={0} | all-to-all | bytes 1966080 | tf_op jit(solution)/shard_map/all_to_all | solution.py:155
  351.9 5.6 %fusion.92 = (f32[4,32]{1,0:T(4,128)S(1)}, f32[4,32]{1,0:T(4,128)S(1)}, f32[4,32,1280]{2,1,0:T(8,128)S(1)}) fusion(f32[4,32]{1,0:T(4,128)S(1)} %add_rsqrt_fusion, f32[4,32]{1,0:T(4,128)S(1)} %broadcast_multiply_fusion.2, bf16[4,32,1280]{2,1,0:T(8,128)(2,1)S(1)} %copy-done.8, f32[1280]{0:T(1024)S(1)} %copy-done.14, ...), kind=kOutput, calls=%fused_computation.98 | convolution fusion | flops 1259437824 | bytes 11803648 | tf_op jit(solution)/shard_map/ehpc,hcd->epd/dot_general | solution.py:156
  357.5 0.5 multiply_reduce_fusion.3
  358.1 0.6 broadcast_in_dim.24
  358.7 4.2 %all-to-all-start.8 = ((f32[32,1,12]{2,1,0:T(1,128)}), f32[32,1,12]{2,1,0:T(1,128)S(1)}, u32[]{:S(2)}, u32[]{:S(2)}) async-start(f32[32,1,12]{2,1,0:T(1,128)} %broadcast_in_dim.24), calls=%async_computation.8 | async-start | bytes 32768 | tf_op jit(solution)/shard_map/all_to_all | solution.py:14
  362.9 6.9 %all-to-all-done.8 = f32[32,1,12]{2,1,0:T(1,128)S(1)} async-done(((f32[32,1,12]{2,1,0:T(1,128)}), f32[32,1,12]{2,1,0:T(1,128)S(1)}, u32[]{:S(2)}, u32[]{:S(2)}) %all-to-all-start.8) | async-done | bytes 1568 | tf_op jit(solution)/shard_map/all_to_all | solution.py:14
  369.9 1.0 add_multiply_fusion
  (70 shorter events, 1.2 us)
Async XLA Ops:
  6.5 113.8 %all-gather.3.cloned.1.call-start = ((), (), s32[]{:S(2)}) async-start(), calls=%async_computation.9 | async-start | bytes 11059200 | tf_op jit(solution)/shard_map/all_gather | solution.py:121
  8.6 118.9 %copy-start.7 = (bf16[4,32,1280]{2,1,0:T(8,128)(2,1)}, bf16[4,32,1280]{2,1,0:T(8,128)(2,1)S(1)}, u32[]{:S(2)}) copy-start(bf16[4,32,1280]{2,1,0:T(8,128)(2,1)S(1)} %get-tuple-element.285) | copy-start | bytes 983044
  128.6 37.3 %all-to-all-start = ((bf16[4,16,32,240]{3,2,0,1:T(8,128)(2,1)}), bf16[4,16,32,240]{3,2,0,1:T(8,128)(2,1)S(1)}, u32[]{:S(2)}, u32[]{:S(2)}) async-start(bf16[4,16,32,240]{3,2,0,1:T(8,128)(2,1)} %copy.161), calls=%async_computation | async-start | bytes 2097152 | tf_op jit(solution)/shard_map/all_to_all | solution.py:132
  132.6 100.5 %all-gather.5.cloned.1.call-start = ((), (), s32[]{:S(2)}) async-start(), calls=%async_computation.10 | async-start | bytes 3686400 | tf_op jit(solution)/shard_map/all_gather | solution.py:122
  166.9 24.7 %all-to-all-start.1 = ((bf16[32,2,32,240]{3,2,1,0:T(8,128)(2,1)}), bf16[32,2,32,240]{3,2,1,0:T(8,128)(2,1)S(1)}, u32[]{:S(2)}, u32[]{:S(2)}) async-start(bf16[32,2,32,240]{3,2,1,0:T(8,128)(2,1)} %bitcast.10), calls=%async_computation.1 | async-start | bytes 2097152 | tf_op jit(solution)/shard_map/all_to_all | solution.py:133
  198.2 37.8 %copy-start.2 = (bf16[2,1024,80]{1,2,0:T(8,128)(2,1)}, bf16[2,1024,80]{1,2,0:T(8,128)(2,1)S(1)}, u32[]{:S(2)}) copy-start(bf16[2,1024,80]{1,2,0:T(8,128)(2,1)S(1)} %get-tuple-element.468) | copy-start | bytes 983044
  198.3 34.9 %copy-start.4 = (f32[4,32,1280]{2,1,0:T(8,128)S(1)}, f32[4,32,1280]{2,1,0:T(8,128)}, u32[]{:S(2)}) copy-start(f32[4,32,1280]{2,1,0:T(8,128)} %param.14) | copy-start | bytes 1966084
  198.3 34.9 %copy-start.13 = (bf16[4,32,1280]{2,1,0:T(8,128)(2,1)S(1)}, bf16[4,32,1280]{2,1,0:T(8,128)(2,1)}, u32[]{:S(2)}) copy-start(bf16[4,32,1280]{2,1,0:T(8,128)(2,1)} %param.13) | copy-start | bytes 983044
  233.2 3.0 copy-start.6
  236.2 1.5 copy-start.11
  256.3 19.6 %all-to-all-start.5 = ((bf16[32,2,32,80]{3,2,1,0:T(8,128)(2,1)}), bf16[32,2,32,80]{3,2,1,0:T(8,128)(2,1)S(1)}, u32[]{:S(2)}, u32[]{:S(2)}) async-start(bf16[32,2,32,80]{3,2,1,0:T(8,128)(2,1)} %bitcast.34), calls=%async_computation.5 | async-start | bytes 1048576 | tf_op jit(solution)/shard_map/all_to_all | solution.py:150
  278.1 2.9 copy-start.3
  278.1 2.9 copy-start.9
  278.9 2.1 copy-start
  282.5 2.2 copy-start.1
  282.5 2.2 copy-start.10
  286.5 2.9 copy-start.3
  286.5 2.9 copy-start.9
  287.3 2.1 copy-start
  291.0 2.2 copy-start.1
  291.0 2.2 copy-start.10
  320.0 31.9 %copy-start.8 = (bf16[4,32,1280]{2,1,0:T(8,128)(2,1)S(1)}, bf16[4,32,1280]{2,1,0:T(8,128)(2,1)}, u32[]{:S(2)}) copy-start(bf16[4,32,1280]{2,1,0:T(8,128)(2,1)} %copy-done.7) | copy-start | bytes 983044
  320.0 31.9 %copy-start.14 = (f32[1280]{0:T(1024)S(1)}, f32[1280]{0:T(1024)}, u32[]{:S(2)}) copy-start(f32[1280]{0:T(1024)} %param.16) | copy-start | bytes 15364
  351.9 5.6 %copy-start.5 = (f32[4,32,1280]{2,1,0:T(8,128)S(1)}, f32[4,32,1280]{2,1,0:T(8,128)}, u32[]{:S(2)}) copy-start(f32[4,32,1280]{2,1,0:T(8,128)} %param.14) | copy-start | bytes 1966084
  351.9 5.6 %copy-start.12 = (f32[4,32,1280]{2,1,0:T(8,128)S(1)}, f32[4,32,1280]{2,1,0:T(8,128)}, u32[]{:S(2)}) copy-start(f32[4,32,1280]{2,1,0:T(8,128)} %copy-done.11) | copy-start | bytes 1966084
  351.9 17.9 %copy-start.15 = (f32[32]{0:T(128)S(1)}, f32[32]{0:T(128)}, u32[]{:S(2)}) copy-start(f32[32]{0:T(128)} %param.20) | copy-start | bytes 388
  351.9 17.9 %copy-start.16 = (f32[32]{0:T(128)S(1)}, f32[32]{0:T(128)}, u32[]{:S(2)}) copy-start(f32[32]{0:T(128)} %param.21) | copy-start | bytes 388
  358.7 11.1 %all-to-all-start.8 = ((f32[32,1,12]{2,1,0:T(1,128)}), f32[32,1,12]{2,1,0:T(1,128)S(1)}, u32[]{:S(2)}, u32[]{:S(2)}) async-start(f32[32,1,12]{2,1,0:T(1,128)} %broadcast_in_dim.24), calls=%async_computation.8 | async-start | bytes 32768 | tf_op jit(solution)/shard_map/all_to_all | solution.py:14
Sparse Core Ops, SparseCore 0:
  9.1 111.2 all-gather.2
  135.2 55.1 all-gather.4
where the time goes:
time: 378 us
  waiting for transfers between devices  180 us (48%)
  blocking collectives  104 us (28%)
  matrix products  33.9 us (9%)
  starting transfers between devices  24 us (6%)
  local copies, waits for them, and re-layouts  14.4 us (4%)
  between operations  13.8 us (4%)
  other arithmetic  6.82 us (2%)
    all_gather x1, waiting for transfers between devices, on_device(): lax.all_gather(w_qkv, 'head', axis=0, tiled=True)  112 us
    all_to_all x1, waiting for transfers between devices, on_device(): lax.all_to_all(packed_own, 'head', split_axis=1, concat_axis=0, tiled=True)  32.5 us
    all_to_all x1, blocking collectives, on_device(): lax.all_to_all(grad_tokens, 'head', split_axis=0, concat_axis=1, tiled=True)  31.6 us
    all_to_all x1, blocking collectives, on_device(): lax.all_to_all(grad_packed[None], 'seq', split_axis=2, concat_axis=0, til...  20.7 us
    all_to_all x1, blocking collectives, on_device(): lax.all_to_all(returned, 'head', split_axis=0, concat_axis=1, tiled=True)  19.2 us
    all_to_all x1, blocking collectives, on_device(): lax.all_to_all(grad_own, 'head', split_axis=1, concat_axis=0, tiled=True)  17.7 us
    all_to_all x1, waiting for transfers between devices, on_device(): lax.all_to_all(packed, 'seq', split_axis=0, concat_axis=2, tiled=True)[0]  17 us
    all_to_all x1, blocking collectives, on_device(): lax.all_to_all(output[None], 'seq', split_axis=2, concat_axis=0, tiled=True)  15 us
  transfers between devices with their start and end apart: 6, of which 5 were waited for; matrix products, arithmetic and copies ran while one was open for 3% of the time, Pallas kernels for 0%

commit v1 on v0

v1 whole, which is shorter than its diff:
```python
import functools
import math

import jax
import jax.numpy as jnp
from jax import lax
from jax.experimental import pallas as pl
from jax.experimental.pallas import tpu as pltpu
from jax.sharding import PartitionSpec as P

norm_epsilon = 1e-06
layer_epsilon = 1e-06

F32 = jnp.float32
BF16 = jnp.bfloat16
NT = (((1,), (1,)), ((), ()))
NN = (((1,), (0,)), ((), ()))
TN = (((0,), (0,)), ((), ()))

IMAGES = 4
ROWS = 4
COLS = 4
PLANES = 8
SEQ = 32
BLOCK = 32
WIDTH = 1280
HD = 80
PAD = 128
CHUNK = 40
NB = 256
NSTEPS = WIDTH // NB
TILE = 256


def dot(a, b, dims):
    return lax.dot_general(a, b, dims, preferred_element_type=F32)


def shard_offset(x, c):
    other = 8 - x - 4 * (1 - (x + 3) // 4)
    return (1 - c) * x + c * other


def kernel(
    pe, pert, tgt, gain, bias, w_own, wo_own, rad, stp, out,
    H, Wp, W2, WO, normed, inv, HS, Q, K, V, O, OR, LSE, GS, GO, GQ, GP, GP2,
    RES, PF, PB, R1L, R1R, S2L, S2R, R2L, R2R, YS, YR, SC, SCR,
    s_wz, r_wz, s_wy, r_wyl, r_wyr, r_wyy, s_hy, r_hy, s_hx, r_hxl, r_hxr, r_hxy, r_hxz,
    s_hd, r_hd, s_wo, r_wo, s_wod, r_wod, l_wo, s_wd, r_wd, s_oa, r_oa, s_ga, r_ga,
    s_gp, r_gp, s_r1, r_r1l, r_r1r, s_r2, r_r2l, r_r2r, s_ry, r_ry, s_sc, r_sc,
):
    s = lax.axis_index("seq")
    z = lax.axis_index("head")
    y = s // 8
    x = (s // 2) % 4
    c = s % 2
    k8 = s % 8

    def at(yy, xx, cc):
        return (yy * 4 + xx) * 2 + cc

    right = at(y, (x + 1) % 4, c)
    left = at(y, (x + 3) % 4, c)
    down = at((y + 1) % 4, x, c)
    up = at((y + 3) % 4, x, c)
    partner = at(y, x, 1 - c)

    def send(src, dst, ssem, rsem, **where):
        copy = pltpu.make_async_remote_copy(
            src_ref=src, dst_ref=dst, send_sem=ssem, recv_sem=rsem,
            device_id=where, device_id_type=pl.DeviceIdType.MESH,
        )
        copy.start()

    def arrived(ref, sem):
        pltpu.make_async_copy(ref, ref, sem).wait()

    barrier = pltpu.get_barrier_semaphore()

    @pl.loop(1, SEQ)
    def _(d):
        pl.semaphore_signal(
            barrier, inc=1, device_id={"seq": (s + d) % SEQ}, device_id_type=pl.DeviceIdType.MESH
        )

    @pl.loop(1, PLANES)
    def _(d):
        pl.semaphore_signal(
            barrier, inc=1, device_id={"head": (z + d) % PLANES},
            device_id_type=pl.DeviceIdType.MESH,
        )

    own_wo = pltpu.make_async_copy(wo_own, WO.at[z, :, pl.ds(0, HD)], l_wo)
    own_wo.start()

    @pl.loop(0, 6)
    def _(t):
        Wp[t, HD:PAD, :] = jnp.zeros((PAD - HD, WIDTH), BF16)

    @pl.loop(0, 16)
    def _(t):
        WO[t // 2, t % 2, HD:PAD, :] = jnp.zeros((PAD - HD, WIDTH), BF16)

    def layer_norm(image):
        mixed = pe[image].astype(F32) + pert[image]
        rounded = mixed.astype(BF16).astype(F32)
        center = rounded - jnp.mean(rounded, axis=-1, keepdims=True)
        variance = jnp.mean(center * center, axis=-1, keepdims=True)
        inverse = lax.rsqrt(variance + layer_epsilon)
        unit = center * inverse
        normed[image] = unit
        inv[image] = jnp.broadcast_to(inverse, (BLOCK, PAD))
        RES[image] = mixed - tgt[image].astype(F32)
        return (unit * gain[...] + bias[...]).astype(BF16)

    @pl.loop(1, ROWS)
    def _(d):
        image = (y + d) % 4
        HS[image] = layer_norm(image)

    H[y, x, c] = layer_norm(y)

    pl.semaphore_wait(barrier, SEQ - 1 + PLANES - 1)

    offset = shard_offset(x, c)
    target = (z + 8 - offset) % 8

    def chunk(yy, j):
        u = 3 * yy + j
        return Wp.at[u // 2, pl.ds(pl.multiple_of(CHUNK * (u % 2), 8), CHUNK)]

    for j in range(3):
        @pl.when(offset == 0)
        def _():
            pltpu.make_async_copy(w_own.at[3 * y + j], chunk(y, j), r_wz.at[j]).start()

        @pl.when(offset != 0)
        def _():
            send(w_own.at[3 * y + j], chunk(y, j), s_wz, r_wz.at[j], head=target)

    @pl.loop(1, ROWS)
    def _(d):
        image = (y + d) % 4
        send(HS.at[image], H.at[y, x, c], s_hy, r_hy.at[d - 1], seq=at(image, x, c))

    def spread(d):
        yy = (y + d) % 4
        block = H.at[yy, x, c]
        send(block, block, s_hx, r_hxl.at[d], seq=right)
        send(block, block, s_hx, r_hxr.at[d], seq=left)
        send(block, block, s_hd, r_hd.at[d * 4], seq=partner)

    spread(0)

    @pl.loop(1, ROWS)
    def _(d):
        arrived(H.at[(y + d) % 4, x, c], r_hy.at[3 - d])
        spread(d)

    for j in range(3):
        arrived(chunk(y, j), r_wz.at[j])
        send(chunk(y, j), chunk(y, j), s_wy, r_wyl.at[j], seq=down)
        send(chunk(y, j), chunk(y, j), s_wy, r_wyr.at[j], seq=up)

    @pl.loop(1, PLANES)
    def _(d):
        send(
            wo_own.at[c], WO.at[z, c, pl.ds(0, HD)], s_wo, r_wo.at[d],
            head=(z + d) % 8,
        )

    @pl.loop(0, ROWS)
    def _(d):
        yy = (y + d) % 4
        from_left = H.at[yy, (x + 3) % 4, c]
        arrived(from_left, r_hxl.at[d])
        upper = H.at[yy, (x + 3) % 4, c, pl.ds(0, 16)]
        send(upper, upper, s_hx, r_hxy.at[d], seq=right)
        send(from_left, from_left, s_hd, r_hd.at[d * 4 + 1], seq=partner)
        from_right = H.at[yy, (x + 1) % 4, c]
        arrived(from_right, r_hxr.at[d])
        lower = H.at[yy, (x + 1) % 4, c, pl.ds(16, 16)]
        send(lower, lower, s_hx, r_hxz.at[d], seq=left)
        send(from_right, from_right, s_hd, r_hd.at[d * 4 + 2], seq=partner)

    yu, yd, yo = (y + 3) % 4, (y + 1) % 4, (y + 2) % 4
    for j in range(3):
        arrived(chunk(yu, j), r_wyl.at[j])
        if j != 1:
            send(chunk(yu, j), chunk(yu, j), s_wy, r_wyy.at[j], seq=down)
        arrived(chunk(yd, j), r_wyr.at[j])
        if j == 1:
            send(chunk(yd, j), chunk(yd, j), s_wy, r_wyy.at[j], seq=up)

    @pl.loop(0, ROWS)
    def _(d):
        yy, xx = (y + d) % 4, (x + 2) % 4
        arrived(H.at[yy, xx, c, pl.ds(0, 16)], r_hxy.at[d])
        arrived(H.at[yy, xx, c, pl.ds(16, 16)], r_hxz.at[d])
        send(H.at[yy, xx, c], H.at[yy, xx, c], s_hd, r_hd.at[d * 4 + 3], seq=partner)

    for j in range(3):
        arrived(chunk(yo, j), r_wyy.at[j])

    send(Wp, W2, s_wd, r_wd, seq=partner)

    @pl.loop(0, ROWS)
    def _(d):
        yy = (y + d) % 4
        arrived(H.at[yy, x, 1 - c], r_hd.at[d * 4])
        arrived(H.at[yy, (x + 3) % 4, 1 - c], r_hd.at[d * 4 + 1])
        arrived(H.at[yy, (x + 1) % 4, 1 - c], r_hd.at[d * 4 + 2])
        arrived(H.at[yy, (x + 2) % 4, 1 - c], r_hd.at[d * 4 + 3])

    @pl.loop(0, 4)
    def _(t):
        rows = pl.ds(pl.multiple_of(t * 256, 256), 256)
        tokens = H[t].reshape(256, WIDTH)
        packed = dot(tokens, Wp[...].reshape(6 * PAD, WIDTH), NT).astype(BF16)
        for h in range(2):
            Q[h, rows] = packed[:, (3 * h) * PAD : (3 * h + 1) * PAD]
            K[h, rows] = packed[:, (3 * h + 1) * PAD : (3 * h + 2) * PAD]
            V[h, rows] = packed[:, (3 * h + 2) * PAD : (3 * h + 3) * PAD]

    scale = 1.0 / math.sqrt(HD)

    @pl.loop(0, 8)
    def _(t):
        h, row = t // 4, t % 4
        rows = pl.ds(pl.multiple_of(row * TILE, TILE), TILE)
        scores = dot(Q[h, rows], K[h], NT) * scale
        top = jnp.max(scores, axis=-1, keepdims=True)
        grown = jnp.exp(scores - top)
        total = jnp.sum(grown, axis=-1, keepdims=True)
        weights = (grown * (1.0 / total)).astype(BF16)
        part = dot(weights, V[h], NN).astype(BF16)
        O[h, row] = part.reshape(8, BLOCK, PAD)
        column = jnp.broadcast_to(top + jnp.log(total), (TILE, PAD))
        LSE[h, :, rows] = jnp.transpose(column)[0:8]

        @pl.loop(0, 8)
        def _(k):
            dest = row * 8 + k

            @pl.when(dest != s)
            def _():
                send(O.at[h, row, k], OR.at[h, y, k8], s_oa, r_oa, seq=dest)

    for h in range(2):
        OR[h, y, k8] = O[h, y, k8]

    @pl.loop(1, PLANES)
    def _(d):
        plane = (z + 8 - d) % 8
        piece = WO.at[plane, c, pl.ds(0, HD)]
        arrived(piece, r_wo.at[d])
        send(piece, piece, s_wod, r_wod.at[d], seq=partner)

    own_wo.wait()

    @pl.loop(1, PLANES)
    def _(d):
        plane = (z + 8 - d) % 8
        arrived(WO.at[plane, 1 - c, pl.ds(0, HD)], r_wod.at[d])

    flat_or = OR.reshape(64, BLOCK, PAD)
    arrived(flat_or.at[pl.ds(0, 62)], r_oa)

    @pl.loop(0, 8)
    def _(k):
        kk = (z + shard_offset((k // 2), k % 2)) % 8
        heads = jnp.concatenate([OR[h, :, k].reshape(128, PAD) for h in range(2)], axis=-1)
        branch = dot(heads, WO[kk].reshape(2 * PAD, WIDTH), NN)
        RES[...] += branch.reshape(IMAGES, BLOCK, WIDTH)

    @pl.loop(0, 8)
    def _(k):
        kk = (z + shard_offset((k // 2), k % 2)) % 8
        half = RES[...].reshape(128, WIDTH).astype(BF16)
        back = dot(half, WO[kk].reshape(2 * PAD, WIDTH), NT).astype(BF16)
        for h in range(2):
            GS[h, :, k] = back[:, h * PAD : (h + 1) * PAD].reshape(IMAGES, BLOCK, PAD)

        @pl.loop(0, IMAGES)
        def _(i):
            dest = i * 8 + k

            @pl.when(dest != s)
            def _():
                for h in range(2):
                    send(GS.at[h, i, k], GO.at[h, s], s_ga, r_ga, seq=dest)

    for h in range(2):
        GO[h, s] = GS[h, y, k8]

    flat_go = GO.reshape(64, BLOCK, PAD)
    arrived(flat_go.at[pl.ds(0, 62)], r_ga)

    @pl.loop(0, 8)
    def _(t):
        h, row = t // 4, t % 4
        rows = pl.ds(pl.multiple_of(row * TILE, TILE), TILE)
        queries = Q[h]
        grads = GO[h].reshape(1024, PAD)
        outputs = O[h].reshape(1024, PAD)
        products = grads.astype(F32) * outputs.astype(F32)
        row_dot = jnp.sum(jnp.transpose(products), axis=0, keepdims=True)
        scores = dot(K[h, rows], queries, NT) * scale
        weights = jnp.exp(scores - LSE[h, 0:1])
        grad_values = dot(weights.astype(BF16), grads, NN)
        grad_weights = dot(V[h, rows], grads, NT)
        grad_scores = (weights * (grad_weights - row_dot) * scale).astype(BF16)
        grad_keys = dot(grad_scores, queries, NN)
        grad_query = dot(grad_scores, K[h, rows], TN)

        @pl.when(row == 0)
        def _():
            GQ[...] = grad_query

        @pl.when(row != 0)
        def _():
            GQ[...] += grad_query

        def store(block_row, kind, value):
            lanes = pl.ds(pl.multiple_of((h * 3 + kind) * PAD, PAD), PAD)
            parts = value.astype(BF16).reshape(4, 2, BLOCK, PAD)
            for cc in range(2):
                GP[cc, block_row, :, :, lanes] = parts[:, cc]

        store(row, 1, grad_keys)
        store(row, 2, grad_values)

        @pl.when(row == 3)
        def _():
            for r in range(4):
                store(r, 0, GQ[r * TILE : (r + 1) * TILE])
            lanes = pl.ds(pl.multiple_of(h * 3 * PAD, PAD), 3 * PAD)
            send(
                GP.at[1 - c, :, :, :, lanes], GP2.at[:, :, :, lanes], s_gp, r_gp.at[h], seq=partner
            )

    arrived(W2, r_wd)
    for h in range(2):
        arrived(GP2.at[:, :, :, h * 3 * PAD : (h + 1) * 3 * PAD], r_gp.at[h])

    xr, xl, xo = (x + 1) % 4, (x + 3) % 4, (x + 2) % 4

    def lanes_of(n):
        return pl.ds(pl.multiple_of(n * NB, NB), NB)

    @pl.loop(0, NSTEPS)
    def _(n):
        lanes = lanes_of(n)
        mine = GP[c].reshape(512, 6 * PAD)
        other = GP2[...].reshape(512, 6 * PAD)
        part = dot(mine, Wp[:, :, lanes].reshape(6 * PAD, NB), NN)
        part = part + dot(other, W2[:, :, lanes].reshape(6 * PAD, NB), NN)
        part = part.reshape(4, 4, BLOCK, NB)
        PF[:, :, :, lanes] = part
        PB[:, :, lanes] = PF[:, xo, :, lanes].astype(BF16)
        send(PB.at[:, pl.ds(0, 16), lanes], R1L.at[:, :, lanes], s_r1, r_r1l.at[n], seq=right)
        send(PB.at[:, pl.ds(16, 16), lanes], R1R.at[:, :, lanes], s_r1, r_r1r.at[n], seq=left)

    @pl.loop(0, NSTEPS)
    def _(n):
        lanes = lanes_of(n)
        arrived(R1L.at[:, :, lanes], r_r1l.at[n])
        S2R[:, 0:16, lanes] = (
            PF[:, xr, 0:16, lanes] + R1L[:, :, lanes].astype(F32)
        ).astype(BF16)
        S2R[:, 16:32, lanes] = PF[:, xr, 16:32, lanes].astype(BF16)
        send(S2R.at[:, :, lanes], R2L.at[:, :, lanes], s_r2, r_r2l.at[n], seq=right)
        arrived(R1R.at[:, :, lanes], r_r1r.at[n])
        S2L[:, 16:32, lanes] = (
            PF[:, xl, 16:32, lanes] + R1R[:, :, lanes].astype(F32)
        ).astype(BF16)
        S2L[:, 0:16, lanes] = PF[:, xl, 0:16, lanes].astype(BF16)
        send(S2L.at[:, :, lanes], R2R.at[:, :, lanes], s_r2, r_r2r.at[n], seq=left)

    @pl.loop(0, NSTEPS)
    def _(n):
        lanes = lanes_of(n)
        arrived(R2L.at[:, :, lanes], r_r2l.at[n])
        arrived(R2R.at[:, :, lanes], r_r2r.at[n])
        total = PF[:, x, :, lanes] + R2L[:, :, lanes].astype(F32) + R2R[:, :, lanes].astype(F32)
        YS[:, :, lanes] = total.astype(BF16)
        for d in range(1, 4):
            send(
                YS.at[(y + d) % 4, :, lanes], YR.at[y, :, lanes], s_ry, r_ry.at[d - 1, n],
                seq=at((y + d) % 4, x, c),
            )

    YR[y] = YS[y]

    @pl.loop(0, NSTEPS)
    def _(n):
        for d in range(1, 4):
            arrived(YR.at[(y + d) % 4, :, lanes_of(n)], r_ry.at[3 - d, n])

    lane = lax.broadcasted_iota(jnp.int32, (8, PAD), 1)
    line = lax.broadcasted_iota(jnp.int32, (8, PAD), 0)

    def total_of(value):
        return jnp.sum(jnp.sum(value, axis=0, keepdims=True), axis=1, keepdims=True)

    sums = jnp.zeros((8, PAD), F32)
    for i in range(IMAGES):
        scaled = YR[i].astype(F32) * gain[...]
        unit = normed[i]
        first = jnp.mean(scaled, axis=-1, keepdims=True)
        second = jnp.mean(scaled * unit, axis=-1, keepdims=True)
        gradient = RES[i] + (scaled - first - unit * second) * inv[i][:, 0:1]
        RES[i] = gradient
        current = pert[i]
        for j, value in enumerate((gradient * gradient, current * gradient, current * current)):
            sums = jnp.where((line == i) & (lane == j), total_of(value), sums)
    SC[...] = sums
    SCR[s] = sums

    @pl.loop(1, SEQ)
    def _(d):
        send(SC, SCR.at[s], s_sc, r_sc, seq=(s + d) % SEQ)

    arrived(SCR.at[pl.ds(0, SEQ - 1)], r_sc)
    sums = jnp.sum(SCR[...], axis=0)

    for i in range(IMAGES):
        grad_square = sums[i : i + 1, 0:1]
        cross = sums[i : i + 1, 1:2]
        own = sums[i : i + 1, 2:3]
        factor = stp[z * IMAGES + i] * lax.rsqrt(grad_square + norm_epsilon)
        stepped_square = own + 2.0 * factor * cross + factor * factor * grad_square
        shrink = jnp.minimum(1.0, rad[z * IMAGES + i] * lax.rsqrt(stepped_square + norm_epsilon))
        out[i] = (pert[i] + factor * RES[i]) * shrink

    @pl.when(offset != 0)
    def _():
        for j in range(3):
            arrived(w_own.at[j], s_wz)

    for j in range(9):
        arrived(w_own.at[j], s_wy)
    arrived(HS.at[pl.ds(0, 3)], s_hy)
    arrived(H.at[0, :, :].reshape(8, BLOCK, WIDTH), s_hx)
    arrived(H.at[0, pl.ds(0, 2)].reshape(4, BLOCK, WIDTH), s_hx)
    arrived(H.at[pl.ds(0, 2)].reshape(16, BLOCK, WIDTH), s_hd)
    arrived(Wp, s_wd)
    for j in range(7):
        arrived(wo_own.at[0], s_wo)
        arrived(wo_own.at[0], s_wod)
    arrived(flat_or.at[pl.ds(0, 62)], s_oa)
    arrived(flat_go.at[pl.ds(0, 62)], s_ga)
    arrived(GP2, s_gp)
    arrived(PB, s_r1)
    arrived(S2R, s_r2)
    arrived(S2L, s_r2)
    arrived(YS.at[pl.ds(0, 3)], s_ry)
    arrived(SCR.at[pl.ds(0, SEQ - 1)], s_sc)


def on_device(patch_embed, perturbation, target, ln_gain, ln_bias, w_qkv, w_out, radius, step_size):
    vmem = pl.BlockSpec(memory_space=pltpu.VMEM)
    smem = pl.BlockSpec(memory_space=pltpu.SMEM)
    anywhere = pl.BlockSpec(memory_space=pl.ANY)
    dma = pltpu.SemaphoreType.DMA
    V = pltpu.VMEM
    scratch = [
        V((4, 4, 2, BLOCK, WIDTH), BF16),
        V((6, PAD, WIDTH), BF16),
        V((6, PAD, WIDTH), BF16),
        V((PLANES, 2, PAD, WIDTH), BF16),
        V((IMAGES, BLOCK, WIDTH), F32),
        V((IMAGES, BLOCK, PAD), F32),
        V((IMAGES, BLOCK, WIDTH), BF16),
        V((2, 1024, PAD), BF16),
        V((2, 1024, PAD), BF16),
        V((2, 1024, PAD), BF16),
        V((2, 4, 8, BLOCK, PAD), BF16),
        V((2, 4, 8, BLOCK, PAD), BF16),
        V((2, 8, 1024), F32),
        V((2, 4, 8, BLOCK, PAD), BF16),
        V((2, 32, BLOCK, PAD), BF16),
        V((1024, PAD), F32),
        V((2, 4, 4, BLOCK, 6 * PAD), BF16),
        V((4, 4, BLOCK, 6 * PAD), BF16),
        V((IMAGES, BLOCK, WIDTH), F32),
        V((4, 4, BLOCK, WIDTH), F32),
        V((4, BLOCK, WIDTH), BF16),
        V((4, 16, WIDTH), BF16),
        V((4, 16, WIDTH), BF16),
        V((4, BLOCK, WIDTH), BF16),
        V((4, BLOCK, WIDTH), BF16),
        V((4, BLOCK, WIDTH), BF16),
        V((4, BLOCK, WIDTH), BF16),
        V((4, BLOCK, WIDTH), BF16),
        V((4, BLOCK, WIDTH), BF16),
        V((8, PAD), F32),
        V((SEQ, 8, PAD), F32),
        dma, dma((3,)), dma, dma((3,)), dma((3,)), dma((3,)),
        dma, dma((3,)), dma, dma((4,)), dma((4,)), dma((4,)), dma((4,)),
        dma, dma((16,)),
        dma, dma((8,)), dma, dma((8,)), dma,
        dma, dma,
        dma, dma, dma, dma,
        dma, dma((2,)),
        dma, dma((NSTEPS,)), dma((NSTEPS,)),
        dma, dma((NSTEPS,)), dma((NSTEPS,)),
        dma, dma((3, NSTEPS)),
        dma, dma,
    ]
    return pl.pallas_call(
        kernel,
        out_shape=jax.ShapeDtypeStruct(perturbation.shape, F32),
        in_specs=[vmem, vmem, vmem, vmem, vmem, anywhere, anywhere, smem, smem],
        out_specs=vmem,
        scratch_shapes=scratch,
        compiler_params=pltpu.CompilerParams(
            collective_id=0, has_side_effects=True, vmem_limit_bytes=62 * 1024 * 1024
        ),
    )(
        patch_embed,
        perturbation,
        target,
        ln_gain.reshape(1, -1),
        ln_bias.reshape(1, -1),
        w_qkv.reshape(12, CHUNK, WIDTH),
        w_out,
        radius,
        step_size,
    )


def solution(mesh):
    placed = (
        P("head", "seq", None),
        P("head", "seq", None),
        P("head", "seq", None),
        P(),
        P(),
        P("head", None, None),
        P("head", None, None),
        P(),
        P(),
    )
    return jax.shard_map(
        on_device, mesh=mesh, in_specs=placed, out_specs=P("head", "seq", None), check_vma=False
    )
```

time: 378 us -> 116 us (0.31)
  waiting for transfers between devices: 180 us -> 0 us
  Pallas kernels: 0 us -> 111 us
  blocking collectives: 104 us -> 0 us
  matrix products: 33.9 us -> 0 us
  starting transfers between devices: 24 us -> 0 us
  between operations: 13.8 us -> 0.01 us
  local copies, waits for them, and re-layouts: 14.4 us -> 4.54 us
  other arithmetic: 6.82 us -> 0 us
    all_gather x2 -> x0, waiting for transfers between devices: 112 us -> none  [the longest x1 112 us: on_device(): lax.all_gather(w_qkv, 'head', axis=0, tiled=True)]
    pallas_call x0 -> x1, Pallas kernels: none -> 111 us  [on_device(): pl.pallas_call(kernel, out_shape=jax.ShapeDtypeStruct(perturbation.shape,...]
    all_to_all x5 -> x0, blocking collectives: 104 us -> none  [the longest x1 31.6 us: on_device(): lax.all_to_all(grad_tokens, 'head', split_axis=0, concat_axis=1, tiled=True)]
    all_to_all x4 -> x0, waiting for transfers between devices: 67.5 us -> none  [the longest x1 32.5 us: on_device(): lax.all_to_all(packed_own, 'head', split_axis=1, concat_axis=0, tiled=True)]
    dot_general x18 -> x0, matrix products: 33.9 us -> none  [the longest x1 7.11 us: on_device(): jnp.einsum('epd,hcd->ehpc', hidden, qkv_every, preferred_element_type=jnp...]
    all_to_all x4 -> x0, starting transfers between devices: 23.9 us -> none  [the longest x1 8.13 us: on_device(): lax.all_to_all(grad_output, 'seq', split_axis=0, concat_axis=2, tiled=True)]
    while x23 -> x0, local copies, waits for them, and re-layouts: 5.26 us -> none
    reduce_sum x7 -> x0, other arithmetic: 4.37 us -> none  [the longest x2 1.88 us: one_block(): jnp.sum(jnp.exp(scores - row_max), axis=-1, keepdims=True)]
  transfers between devices with their start and end apart: 6 -> 0, of which waited for: 5 -> 0; matrix products, arithmetic and copies ran while one was open for 3% -> 0% of each run, Pallas kernels for 0% -> 0%
where the time goes in v1:
time: 116 us
  Pallas kernels  111 us (96%)
  local copies, waits for them, and re-layouts  4.54 us (4%)
    pallas_call x1, Pallas kernels, on_device(): pl.pallas_call(kernel, out_shape=jax.ShapeDtypeStruct(perturbation.shape,...  111 us

profile of v1, /device:TPU:1, one launch (start us, length us, event | category | flops | bytes accessed | tf_op | source)
XLA Modules:
  0.0 115.7 jit_solution(6022576844776851908)
XLA Ops:
  0.0 1.3 %reshape.9.gain = f32[1,1280]{1,0:T(1,128)} reshape(f32[1280]{0:T(1024)} %param.12) | data formatting | bytes 10240 | tf_op jit(solution)/shard_map/reshape | solution.py:524
  1.3 1.3 %reshape.10.bias = f32[1,1280]{1,0:T(1,128)} reshape(f32[1280]{0:T(1024)} %param.13) | data formatting | bytes 10240 | tf_op jit(solution)/shard_map/reshape | solution.py:525
  2.6 111.2 %shard_map.91 = f32[4,32,1280]{2,1,0:T(8,128)} custom-call(bf16[4,32,1280]{2,1,0:T(8,128)(2,1)} %pe.1, f32[4,32,1280]{2,1,0:T(8,128)} %pert.1, bf16[4,32,1280]{2,1,0:T(8,128)(2,1)} %tgt.1, f32[1,1280]{1,0:T(1,128)} %reshape.9.gain, f32[1,1280]{1,0:T(1,128)} %reshape.10.bias, bf16[12,40,1280]{2,1,0:T(8,128)(2,1)} %bitcast.1, bf16[2,80,1280]{2,1,0:T(8,128)(2,1)} %wo_own.1, ...), custom_call_target="tpu_custom_call" | custom-call | tf_op jit(solution)/shard_map/pallas_call | solution.py:511
  113.7 2.0 %copy.11 = f32[4,32,1280]{2,1,0:T(8,128)} copy(f32[4,32,1280]{2,1,0:T(8,128)} %shard_map.91) | data formatting | bytes 1310720

commit v2 on v1

--- a/solution.py
+++ b/solution.py
@@ -29,6 +29,7 @@
 CHUNK = 40
 NB = 256
 NSTEPS = WIDTH // NB
+CHUNKS = 6
 TILE = 256
 
 
@@ -42,11 +43,12 @@
 
 
 def kernel(
-    pe, pert, tgt, gain, bias, w_own, wo_own, rad, stp, out,
-    H, Wp, W2, WO, normed, inv, HS, Q, K, V, O, OR, LSE, GS, GO, GQ, GP, GP2,
-    RES, PF, PB, R1L, R1R, S2L, S2R, R2L, R2R, YS, YR, SC, SCR,
-    s_wz, r_wz, s_wy, r_wyl, r_wyr, r_wyy, s_hy, r_hy, s_hx, r_hxl, r_hxr, r_hxy, r_hxz,
-    s_hd, r_hd, s_wo, r_wo, s_wod, r_wod, l_wo, s_wd, r_wd, s_oa, r_oa, s_ga, r_ga,
+    pe_in, pert_in, tgt_in, gain_in, bias_in, w_own, wo_own, rad_in, stp_in, grad_out, sums_out,
+    pe, pert, tgt, gain, bias, rad, stp,
+    H, RB, Wp, W2, WO, normed, inv, HS, Q, K, V, O, OR, LSE, DOT, GS, GO, GQ, GP, GP2,
+    RES, RESB, PF, PB, R1L, R1R, S2L, S2R, R2L, R2R, YS, YR, SC, SCR,
+    l_in, l_out, s_rb, r_rb, s_wz, r_wz, s_wy, r_wyl, r_wyr, r_wyy, s_hy, r_hy, s_hx, r_hxl, r_hxr, r_hxy, r_hxz,
+    s_hd, r_hd, s_wo, r_wo, s_woy, r_wol, r_wor, r_woz, s_wod, r_wod, l_wo, s_wd, r_wd, s_oa, r_oa, s_ga, r_ga,
     s_gp, r_gp, s_r1, r_r1l, r_r1r, s_r2, r_r2l, r_r2r, s_ry, r_ry, s_sc, r_sc,
 ):
     s = lax.axis_index("seq")
@@ -74,6 +76,16 @@
 
     def arrived(ref, sem):
         pltpu.make_async_copy(ref, ref, sem).wait()
+
+    loads = [
+        pltpu.make_async_copy(src, dst, l_in.at[i])
+        for i, (src, dst) in enumerate(
+            ((pe_in, pe), (pert_in, pert), (tgt_in, tgt), (gain_in, gain), (bias_in, bias),
+             (rad_in, rad), (stp_in, stp))
+        )
+    ]
+    for load in loads:
+        load.start()
 
     barrier = pltpu.get_barrier_semaphore()
 
@@ -111,7 +123,10 @@
         normed[image] = unit
         inv[image] = jnp.broadcast_to(inverse, (BLOCK, PAD))
         RES[image] = mixed - tgt[image].astype(F32)
-        return (unit * gain[...] + bias[...]).astype(BF16)
+        return (unit * gain[...].reshape(1, WIDTH) + bias[...].reshape(1, WIDTH)).astype(BF16)
+
+    for load in loads:
+        load.wait()
 
     @pl.loop(1, ROWS)
     def _(d):
@@ -125,18 +140,45 @@
     offset = shard_offset(x, c)
     target = (z + 8 - offset) % 8
 
-    def chunk(yy, j):
-        u = 3 * yy + j
-        return Wp.at[u // 2, pl.ds(pl.multiple_of(CHUNK * (u % 2), 8), CHUNK)]
-
-    for j in range(3):
+    half_width = WIDTH // 2
+
+    def chunk(yy, q):
+        u = 3 * yy + q % 3
+        rows = pl.ds(pl.multiple_of(CHUNK * (u % 2), 8), CHUNK)
+        return Wp.at[u // 2, rows, pl.ds((q // 3) * half_width, half_width)]
+
+    def source(q):
+        return w_own.at[3 * y + q % 3, :, pl.ds((q // 3) * half_width, half_width)]
+
+    between = {0: (0, 2), 1: (1, 6), 3: (2, 2), 4: (3, 6)}
+
+    for q in range(CHUNKS):
         @pl.when(offset == 0)
         def _():
-            pltpu.make_async_copy(w_own.at[3 * y + j], chunk(y, j), r_wz.at[j]).start()
-
-        @pl.when(offset != 0)
+            pltpu.make_async_copy(source(q), chunk(y, q), r_wz.at[q]).start()
+
+        if q in between:
+            slot, hop = between[q]
+
+            @pl.when(offset == 4)
+            def _():
+                send(source(q), RB.at[slot], s_wz, r_rb.at[slot], head=(z + hop) % 8)
+
+            @pl.when((offset != 0) & (offset != 4))
+            def _():
+                send(source(q), chunk(y, q), s_wz, r_wz.at[q], head=target)
+        else:
+            @pl.when(offset != 0)
+            def _():
+                send(source(q), chunk(y, q), s_wz, r_wz.at[q], head=target)
+
+    def pass_on(q):
+        slot, hop = between[q]
+
+        @pl.when(offset == 4)
         def _():
-            send(w_own.at[3 * y + j], chunk(y, j), s_wz, r_wz.at[j], head=target)
+            arrived(RB.at[slot], r_rb.at[slot])
+            send(RB.at[slot], chunk(y, q), s_rb, r_wz.at[q], head=(z + hop) % 8)
 
     @pl.loop(1, ROWS)
     def _(d):
@@ -150,27 +192,7 @@
         send(block, block, s_hx, r_hxr.at[d], seq=left)
         send(block, block, s_hd, r_hd.at[d * 4], seq=partner)
 
-    spread(0)
-
-    @pl.loop(1, ROWS)
-    def _(d):
-        arrived(H.at[(y + d) % 4, x, c], r_hy.at[3 - d])
-        spread(d)
-
-    for j in range(3):
-        arrived(chunk(y, j), r_wz.at[j])
-        send(chunk(y, j), chunk(y, j), s_wy, r_wyl.at[j], seq=down)
-        send(chunk(y, j), chunk(y, j), s_wy, r_wyr.at[j], seq=up)
-
-    @pl.loop(1, PLANES)
-    def _(d):
-        send(
-            wo_own.at[c], WO.at[z, c, pl.ds(0, HD)], s_wo, r_wo.at[d],
-            head=(z + d) % 8,
-        )
-
-    @pl.loop(0, ROWS)
-    def _(d):
+    def relay(d):
         yy = (y + d) % 4
         from_left = H.at[yy, (x + 3) % 4, c]
         arrived(from_left, r_hxl.at[d])
@@ -183,26 +205,132 @@
         send(lower, lower, s_hx, r_hxz.at[d], seq=left)
         send(from_right, from_right, s_hd, r_hd.at[d * 4 + 2], seq=partner)
 
+    def from_row(d):
+        arrived(H.at[(y + d) % 4, x, c], r_hy.at[3 - d])
+        spread(d)
+
+    def round_column(j):
+        arrived(chunk(y, j), r_wz.at[j])
+        send(chunk(y, j), chunk(y, j), s_wy, r_wyl.at[j], seq=down)
+        send(chunk(y, j), chunk(y, j), s_wy, r_wyr.at[j], seq=up)
+
+    def ways(plane):
+        odd = plane % 2
+        place = odd * y + (1 - odd) * x
+        return place, odd * down + (1 - odd) * right, odd * up + (1 - odd) * left
+
+    def piece(ref, place, cc):
+        rows = pl.ds(pl.multiple_of(CHUNK * (place % 2), 8), CHUNK)
+        lanes = pl.ds(pl.multiple_of(cc * half_width, PAD), half_width)
+        return ref.at[place // 2, rows, lanes]
+
+    def half_shard(plane, cc):
+        lanes = pl.ds(pl.multiple_of(cc * half_width, PAD), half_width)
+        return WO.at[plane, :, pl.ds(0, HD), lanes]
+
+    def wo_start():
+        place, _, _ = ways(z)
+        mine, there = piece(wo_own, place, c), piece(WO.at[z], place, c)
+        send(mine, there, s_wo, r_wo.at[1], head=(z + 1) % 8)
+        send(mine, there, s_wo, r_wo.at[7], head=(z + 7) % 8)
+
+    def wo_chain(step):
+        for d, ahead, there, last in ((step, 1, step + 1, 4), (8 - step, 7, 7 - step, 5)):
+            if step == 4 and ahead == 7:
+                continue
+            plane = (z + 8 - d) % 8
+            place, _, _ = ways(plane)
+            got = piece(WO.at[plane], place, c)
+            arrived(got, r_wo.at[d])
+            if d != last:
+                send(got, got, s_wo, r_wo.at[there], head=(z + ahead) % 8)
+
+    def wo_first(d):
+        plane = (z + 8 - d) % 8
+        place, after, before = ways(plane)
+        got = piece(WO.at[plane], place, c)
+        send(got, got, s_woy, r_wol.at[d], seq=after)
+        send(got, got, s_woy, r_wor.at[d], seq=before)
+
+    def wo_second(d):
+        plane = (z + 8 - d) % 8
+        place, after, before = ways(plane)
+        shard = WO.at[plane]
+        lower, upper = piece(shard, (place + 3) % 4, c), piece(shard, (place + 1) % 4, c)
+        arrived(lower, r_wol.at[d])
+        arrived(upper, r_wor.at[d])
+        turn = (plane // 2) % 2
+
+        @pl.when(turn == 0)
+        def _():
+            send(lower, lower, s_woy, r_woz.at[d], seq=after)
+
+        @pl.when(turn == 1)
+        def _():
+            send(upper, upper, s_woy, r_woz.at[d], seq=before)
+
+    def wo_third(d):
+        plane = (z + 8 - d) % 8
+        place, _, _ = ways(plane)
+        arrived(piece(WO.at[plane], (place + 2) % 4, c), r_woz.at[d])
+        got = half_shard(plane, c)
+        send(got, got, s_wod, r_wod.at[d], seq=partner)
+
     yu, yd, yo = (y + 3) % 4, (y + 1) % 4, (y + 2) % 4
-    for j in range(3):
-        arrived(chunk(yu, j), r_wyl.at[j])
-        if j != 1:
-            send(chunk(yu, j), chunk(yu, j), s_wy, r_wyy.at[j], seq=down)
-        arrived(chunk(yd, j), r_wyr.at[j])
-        if j == 1:
-            send(chunk(yd, j), chunk(yd, j), s_wy, r_wyy.at[j], seq=up)
-
-    @pl.loop(0, ROWS)
-    def _(d):
+
+    def relay_column(q):
+        arrived(chunk(yu, q), r_wyl.at[q])
+        arrived(chunk(yd, q), r_wyr.at[q])
+        if q % 2 == 0:
+            send(chunk(yu, q), chunk(yu, q), s_wy, r_wyy.at[q], seq=down)
+        else:
+            send(chunk(yd, q), chunk(yd, q), s_wy, r_wyy.at[q], seq=up)
+
+    def far_column(d):
         yy, xx = (y + d) % 4, (x + 2) % 4
         arrived(H.at[yy, xx, c, pl.ds(0, 16)], r_hxy.at[d])
         arrived(H.at[yy, xx, c, pl.ds(16, 16)], r_hxz.at[d])
         send(H.at[yy, xx, c], H.at[yy, xx, c], s_hd, r_hd.at[d * 4 + 3], seq=partner)
 
-    for j in range(3):
-        arrived(chunk(yo, j), r_wyy.at[j])
+    spread(0)
+    wo_start()
+    from_row(1)
+    relay(0)
+    from_row(3)
+    pass_on(0)
+    pass_on(1)
+    from_row(2)
+    round_column(0)
+    round_column(1)
+    relay(1)
+    round_column(2)
+    relay_column(0)
+    relay(3)
+    wo_chain(1)
+    pass_on(3)
+    pass_on(4)
+    relay_column(1)
+    relay(2)
+    round_column(3)
+    relay_column(2)
+    round_column(4)
+    far_column(0)
+    round_column(5)
+    relay_column(3)
+    wo_chain(2)
+    far_column(1)
+    relay_column(4)
+    far_column(3)
+    relay_column(5)
+    far_column(2)
+
+    for q in range(CHUNKS):
+        arrived(chunk(yo, q), r_wyy.at[q])
 
     send(Wp, W2, s_wd, r_wd, seq=partner)
+    wo_chain(3)
+    for d in (1, 7, 2, 6):
+        wo_first(d)
 
     @pl.loop(0, ROWS)
     def _(d):
@@ -211,11 +339,8 @@
         arrived(H.at[yy, (x + 3) % 4, 1 - c], r_hd.at[d * 4 + 1])
         arrived(H.at[yy, (x + 1) % 4, 1 - c], r_hd.at[d * 4 + 2])
         arrived(H.at[yy, (x + 2) % 4, 1 - c], r_hd.at[d * 4 + 3])
-
-    @pl.loop(0, 4)
-    def _(t):
-        rows = pl.ds(pl.multiple_of(t * 256, 256), 256)
-        tokens = H[t].reshape(256, WIDTH)
+        rows = pl.ds(pl.multiple_of(yy * 256, 256), 256)
+        tokens = H[yy].reshape(256, WIDTH)
         packed = dot(tokens, Wp[...].reshape(6 * PAD, WIDTH), NT).astype(BF16)
         for h in range(2):
             Q[h, rows] = packed[:, (3 * h) * PAD : (3 * h + 1) * PAD]
@@ -224,44 +349,59 @@
 
     scale = 1.0 / math.sqrt(HD)
 
-    @pl.loop(0, 8)
-    def _(t):
-        h, row = t // 4, t % 4
+    wo_chain(4)
+    for d in (3, 5, 4):
+        wo_first(d)
+
+    @pl.loop(0, 4)
+    def _(step):
+        row = (y + 3 - step) % 4
+
+        @pl.when(step == 1)
+        def _():
+            for d in (1, 7, 2, 6):
+                wo_second(d)
+
+        @pl.when(step == 2)
+        def _():
+            for d in (3, 5, 4):
+                wo_second(d)
+
+        @pl.when(step == 3)
+        def _():
+            for d in (1, 7, 2, 6):
+                wo_third(d)
+
         rows = pl.ds(pl.multiple_of(row * TILE, TILE), TILE)
-        scores = dot(Q[h, rows], K[h], NT) * scale
-        top = jnp.max(scores, axis=-1, keepdims=True)
-        grown = jnp.exp(scores - top)
-        total = jnp.sum(grown, axis=-1, keepdims=True)
-        weights = (grown * (1.0 / total)).astype(BF16)
-        part = dot(weights, V[h], NN).astype(BF16)
-        O[h, row] = part.reshape(8, BLOCK, PAD)
-        column = jnp.broadcast_to(top + jnp.log(total), (TILE, PAD))
-        LSE[h, :, rows] = jnp.transpose(column)[0:8]
+        for h in range(2):
+            scores = dot(Q[h, rows], K[h], NT) * scale
+            top = jnp.max(scores, axis=-1, keepdims=True)
+            grown = jnp.exp(scores - top)
+            total = jnp.sum(grown, axis=-1, keepdims=True)
+            weights = (grown * (1.0 / total)).astype(BF16)
+            part = dot(weights, V[h], NN).astype(BF16)
+            O[h, row] = part.reshape(8, BLOCK, PAD)
+            column = jnp.broadcast_to(top + jnp.log(total), (TILE, PAD))
+            LSE[h, :, rows] = jnp.transpose(column)[0:8]
 
         @pl.loop(0, 8)
-        def _(k):
+        def _(turn):
+            k = (k8 + 7 - turn) % 8
             dest = row * 8 + k
 
             @pl.when(dest != s)
             def _():
-                send(O.at[h, row, k], OR.at[h, y, k8], s_oa, r_oa, seq=dest)
+                for h in range(2):
+                    send(O.at[h, row, k], OR.at[h, y, k8], s_oa, r_oa, seq=dest)
 
     for h in range(2):
         OR[h, y, k8] = O[h, y, k8]
 
-    @pl.loop(1, PLANES)
-    def _(d):
-        plane = (z + 8 - d) % 8
-        piece = WO.at[plane, c, pl.ds(0, HD)]
-        arrived(piece, r_wo.at[d])
-        send(piece, piece, s_wod, r_wod.at[d], seq=partner)
-
+    for d in (3, 5, 4):
+        wo_third(d)
     own_wo.wait()
-
-    @pl.loop(1, PLANES)
-    def _(d):
-        plane = (z + 8 - d) % 8
-        arrived(WO.at[plane, 1 - c, pl.ds(0, HD)], r_wod.at[d])
+    for d in range(1, PLANES):
+        arrived(half_shard((z + 8 - d) % 8, 1 - c), r_wod.at[d])
 
     flat_or = OR.reshape(64, BLOCK, PAD)
     arrived(flat_or.at[pl.ds(0, 62)], r_oa)
@@ -273,16 +413,19 @@
         branch = dot(heads, WO[kk].reshape(2 * PAD, WIDTH), NN)
         RES[...] += branch.reshape(IMAGES, BLOCK, WIDTH)
 
+    RESB[...] = RES[...].reshape(128, WIDTH).astype(BF16)
+
     @pl.loop(0, 8)
-    def _(k):
+    def _(turn):
+        k = ((x + 3 - turn // 2) % 4) * 2 + turn % 2
         kk = (z + shard_offset((k // 2), k % 2)) % 8
-        half = RES[...].reshape(128, WIDTH).astype(BF16)
-        back = dot(half, WO[kk].reshape(2 * PAD, WIDTH), NT).astype(BF16)
+        back = dot(RESB[...], WO[kk].reshape(2 * PAD, WIDTH), NT).astype(BF16)
         for h in range(2):
             GS[h, :, k] = back[:, h * PAD : (h + 1) * PAD].reshape(IMAGES, BLOCK, PAD)
 
         @pl.loop(0, IMAGES)
-        def _(i):
+        def _(turn):
+            i = (y + 3 - turn) % 4
             dest = i * 8 + k
 
             @pl.when(dest != s)
@@ -296,52 +439,61 @@
     flat_go = GO.reshape(64, BLOCK, PAD)
     arrived(flat_go.at[pl.ds(0, 62)], r_ga)
 
-    @pl.loop(0, 8)
-    def _(t):
-        h, row = t // 4, t % 4
+    for h in range(2):
+        products = GO[h].reshape(1024, PAD).astype(F32) * O[h].reshape(1024, PAD).astype(F32)
+        DOT[h] = jnp.broadcast_to(
+            jnp.sum(jnp.transpose(products), axis=0, keepdims=True), (8, 1024)
+        )
+
+    def store(block_row, h, kind, value):
+        parts = value.astype(BF16).reshape(4, 2, BLOCK, PAD)
+        t = h * 3 + kind
+        for cc in range(2):
+            GP[cc, block_row, :, :, t * PAD : (t + 1) * PAD] = parts[:, cc]
+
+    @pl.loop(0, 4)
+    def _(row):
         rows = pl.ds(pl.multiple_of(row * TILE, TILE), TILE)
-        queries = Q[h]
-        grads = GO[h].reshape(1024, PAD)
-        outputs = O[h].reshape(1024, PAD)
-        products = grads.astype(F32) * outputs.astype(F32)
-        row_dot = jnp.sum(jnp.transpose(products), axis=0, keepdims=True)
-        scores = dot(K[h, rows], queries, NT) * scale
-        weights = jnp.exp(scores - LSE[h, 0:1])
-        grad_values = dot(weights.astype(BF16), grads, NN)
-        grad_weights = dot(V[h, rows], grads, NT)
-        grad_scores = (weights * (grad_weights - row_dot) * scale).astype(BF16)
-        grad_keys = dot(grad_scores, queries, NN)
-        grad_query = dot(grad_scores, K[h, rows], TN)
-
-        @pl.when(row == 0)
-        def _():
-            GQ[...] = grad_query
-
-        @pl.when(row != 0)
-        def _():
-            GQ[...] += grad_query
-
-        def store(block_row, kind, value):
-            lanes = pl.ds(pl.multiple_of((h * 3 + kind) * PAD, PAD), PAD)
-            parts = value.astype(BF16).reshape(4, 2, BLOCK, PAD)
-            for cc in range(2):
-                GP[cc, block_row, :, :, lanes] = parts[:, cc]
-
-        store(row, 1, grad_keys)
-        store(row, 2, grad_values)
-
-        @pl.when(row == 3)
-        def _():
-            for r in range(4):
-                store(r, 0, GQ[r * TILE : (r + 1) * TILE])
-            lanes = pl.ds(pl.multiple_of(h * 3 * PAD, PAD), 3 * PAD)
+        for h in range(2):
+            queries = Q[h]
+            grads = GO[h].reshape(1024, PAD)
+            scores = dot(K[h, rows], queries, NT) * scale
+            weights = jnp.exp(scores - LSE[h, 0:1])
+            grad_values = dot(weights.astype(BF16), grads, NN)
+            grad_weights = dot(V[h, rows], grads, NT)
+            grad_scores = (weights * (grad_weights - DOT[h, 0:1]) * scale).astype(BF16)
+            grad_keys = dot(grad_scores, queries, NN)
+            grad_query = dot(grad_scores, K[h, rows], TN)
+
+            @pl.when(row == 0)
+            def _():
+                GQ[h] = grad_query
+
+            @pl.when(row != 0)
+            def _():
+                GQ[h] += grad_query
+
+            store(row, h, 1, grad_keys)
+            store(row, h, 2, grad_values)
+
+        for h in range(2):
+            lanes = pl.ds((h * 3 + 1) * PAD, 2 * PAD)
             send(
-                GP.at[1 - c, :, :, :, lanes], GP2.at[:, :, :, lanes], s_gp, r_gp.at[h], seq=partner
+                GP.at[1 - c, row, :, :, lanes], GP2.at[row, :, :, lanes], s_gp, r_gp.at[h, row],
+                seq=partner,
             )
+
+    for h in range(2):
+        for r in range(4):
+            store(r, h, 0, GQ[h, r * TILE : (r + 1) * TILE])
+        lanes = pl.ds(h * 3 * PAD, PAD)
+        send(GP.at[1 - c, :, :, :, lanes], GP2.at[:, :, :, lanes], s_gp, r_gp.at[h, 4], seq=partner)
 
     arrived(W2, r_wd)
     for h in range(2):
-        arrived(GP2.at[:, :, :, h * 3 * PAD : (h + 1) * 3 * PAD], r_gp.at[h])
+        for r in range(4):
+            arrived(GP2.at[r, :, :, pl.ds((h * 3 + 1) * PAD, 2 * PAD)], r_gp.at[h, r])
+        arrived(GP2.at[:, :, :, pl.ds(h * 3 * PAD, PAD)], r_gp.at[h, 4])
 
     xr, xl, xo = (x + 1) % 4, (x + 3) % 4, (x + 2) % 4
 
@@ -405,12 +557,13 @@
 
     sums = jnp.zeros((8, PAD), F32)
     for i in range(IMAGES):
-        scaled = YR[i].astype(F32) * gain[...]
+        scaled = YR[i].astype(F32) * gain[...].reshape(1, WIDTH)
         unit = normed[i]
         first = jnp.mean(scaled, axis=-1, keepdims=True)
         second = jnp.mean(scaled * unit, axis=-1, keepdims=True)
         gradient = RES[i] + (scaled - first - unit * second) * inv[i][:, 0:1]
         RES[i] = gradient
+        pltpu.make_async_copy(RES.at[i], grad_out.at[i], l_out.at[i]).start()
         current = pert[i]
         for j, value in enumerate((gradient * gradient, current * gradient, current * current)):
             sums = jnp.where((line == i) & (lane == j), total_of(value), sums)
@@ -423,31 +576,41 @@
 
     arrived(SCR.at[pl.ds(0, SEQ - 1)], r_sc)
     sums = jnp.sum(SCR[...], axis=0)
-
+    column = lax.broadcasted_iota(jnp.int32, (8, 1), 0)
+    step_of, radius_of = jnp.ones((8, 1), F32), jnp.ones((8, 1), F32)
     for i in range(IMAGES):
-        grad_square = sums[i : i + 1, 0:1]
-        cross = sums[i : i + 1, 1:2]
-        own = sums[i : i + 1, 2:3]
-        factor = stp[z * IMAGES + i] * lax.rsqrt(grad_square + norm_epsilon)
-        stepped_square = own + 2.0 * factor * cross + factor * factor * grad_square
-        shrink = jnp.minimum(1.0, rad[z * IMAGES + i] * lax.rsqrt(stepped_square + norm_epsilon))
-        out[i] = (pert[i] + factor * RES[i]) * shrink
+        step_of = jnp.where(column == i, stp[z * IMAGES + i], step_of)
+        radius_of = jnp.where(column == i, rad[z * IMAGES + i], radius_of)
+    grad_square, cross, own = sums[:, 0:1], sums[:, 1:2], sums[:, 2:3]
+    factor = step_of / jnp.sqrt(grad_square + norm_epsilon)
+    stepped_square = own + 2.0 * factor * cross + factor * factor * grad_square
+    shrink = jnp.minimum(1.0, radius_of / jnp.sqrt(stepped_square + norm_epsilon))
+    sums_out[...] = jnp.where(lane == 0, shrink, factor * shrink)
+    for i in range(IMAGES):
+        pltpu.make_async_copy(RES.at[i], grad_out.at[i], l_out.at[i]).wait()
 
     @pl.when(offset != 0)
     def _():
-        for j in range(3):
-            arrived(w_own.at[j], s_wz)
-
-    for j in range(9):
-        arrived(w_own.at[j], s_wy)
+        for q in range(CHUNKS):
+            arrived(source(q), s_wz)
+
+    @pl.when(offset == 4)
+    def _():
+        arrived(RB, s_rb)
+
+    for q in range(CHUNKS):
+        for _ in range(3):
+            arrived(source(q), s_wy)
     arrived(HS.at[pl.ds(0, 3)], s_hy)
     arrived(H.at[0, :, :].reshape(8, BLOCK, WIDTH), s_hx)
     arrived(H.at[0, pl.ds(0, 2)].reshape(4, BLOCK, WIDTH), s_hx)
     arrived(H.at[pl.ds(0, 2)].reshape(16, BLOCK, WIDTH), s_hd)
     arrived(Wp, s_wd)
-    for j in range(7):
-        arrived(wo_own.at[0], s_wo)
-        arrived(wo_own.at[0], s_wod)
+    for d in range(1, PLANES):
+        arrived(piece(wo_own, y, c), s_wo)
+        for _ in range(3):
+            arrived(piece(wo_own, y, c), s_woy)
+        arrived(half_shard(z, c), s_wod)
     arrived(flat_or.at[pl.ds(0, 62)], s_oa)
     arrived(flat_go.at[pl.ds(0, 62)], s_ga)
     arrived(GP2, s_gp)
@@ -460,12 +623,19 @@
 
 def on_device(patch_embed, perturbation, target, ln_gain, ln_bias, w_qkv, w_out, radius, step_size):
     vmem = pl.BlockSpec(memory_space=pltpu.VMEM)
-    smem = pl.BlockSpec(memory_space=pltpu.SMEM)
     anywhere = pl.BlockSpec(memory_space=pl.ANY)
     dma = pltpu.SemaphoreType.DMA
     V = pltpu.VMEM
     scratch = [
+        V(patch_embed.shape, BF16),
+        V(perturbation.shape, F32),
+        V(target.shape, BF16),
+        V(ln_gain.shape, F32),
+        V(ln_bias.shape, F32),
+        pltpu.SMEM(radius.shape, F32),
+        pltpu.SMEM(step_size.shape, F32),
         V((4, 4, 2, BLOCK, WIDTH), BF16),
+        V((4, CHUNK, WIDTH // 2), BF16),
         V((6, PAD, WIDTH), BF16),
         V((6, PAD, WIDTH), BF16),
         V((PLANES, 2, PAD, WIDTH), BF16),
@@ -478,12 +648,14 @@
         V((2, 4, 8, BLOCK, PAD), BF16),
         V((2, 4, 8, BLOCK, PAD), BF16),
         V((2, 8, 1024), F32),
+        V((2, 8, 1024), F32),
         V((2, 4, 8, BLOCK, PAD), BF16),
         V((2, 32, BLOCK, PAD), BF16),
-        V((1024, PAD), F32),
+        V((2, 1024, PAD), F32),
         V((2, 4, 4, BLOCK, 6 * PAD), BF16),
         V((4, 4, BLOCK, 6 * PAD), BF16),
         V((IMAGES, BLOCK, WIDTH), F32),
+        V((IMAGES * BLOCK, WIDTH), BF16),
         V((4, 4, BLOCK, WIDTH), F32),
         V((4, BLOCK, WIDTH), BF16),
         V((4, 16, WIDTH), BF16),
@@ -496,23 +668,27 @@
         V((4, BLOCK, WIDTH), BF16),
         V((8, PAD), F32),
         V((SEQ, 8, PAD), F32),
-        dma, dma((3,)), dma, dma((3,)), dma((3,)), dma((3,)),
+        dma((7,)), dma((IMAGES,)), dma, dma((4,)),
+        dma, dma((CHUNKS,)), dma, dma((CHUNKS,)), dma((CHUNKS,)), dma((CHUNKS,)),
         dma, dma((3,)), dma, dma((4,)), dma((4,)), dma((4,)), dma((4,)),
         dma, dma((16,)),
-        dma, dma((8,)), dma, dma((8,)), dma,
+        dma, dma((8,)), dma, dma((8,)), dma((8,)), dma((8,)), dma, dma((8,)), dma,
         dma, dma,
         dma, dma, dma, dma,
-        dma, dma((2,)),
+        dma, dma((2, 5)),
         dma, dma((NSTEPS,)), dma((NSTEPS,)),
         dma, dma((NSTEPS,)), dma((NSTEPS,)),
         dma, dma((3, NSTEPS)),
         dma, dma,
     ]
-    return pl.pallas_call(
+    gradient, sums = pl.pallas_call(
         kernel,
-        out_shape=jax.ShapeDtypeStruct(perturbation.shape, F32),
-        in_specs=[vmem, vmem, vmem, vmem, vmem, anywhere, anywhere, smem, smem],
-        out_specs=vmem,
+        out_shape=(
+            jax.ShapeDtypeStruct(perturbation.shape, F32),
+            jax.ShapeDtypeStruct((8, PAD), F32),
+        ),
+        in_specs=[anywhere] * 9,
+        out_specs=(anywhere, vmem),
         scratch_shapes=scratch,
         compiler_params=pltpu.CompilerParams(
             collective_id=0, has_side_effects=True, vmem_limit_bytes=62 * 1024 * 1024
@@ -521,13 +697,15 @@
         patch_embed,
         perturbation,
         target,
-        ln_gain.reshape(1, -1),
-        ln_bias.reshape(1, -1),
+        ln_gain,
+        ln_bias,
         w_qkv.reshape(12, CHUNK, WIDTH),
         w_out,
         radius,
         step_size,
     )
+    shrink, factor = sums[:IMAGES, 0:1, None], sums[:IMAGES, 1:2, None]
+    return perturbation * shrink + factor * gradient
 
 
 def solution(mesh):

time: 116 us -> 106 us (0.914)
  Pallas kernels: 111 us -> 103 us
  local copies, waits for them, and re-layouts: 4.54 us -> 0.95 us
  other arithmetic: 0 us -> 2.06 us
    pallas_call x1, Pallas kernels: 111 us -> 103 us  [on_device(): pl.pallas_call(kernel, out_shape=(jax.ShapeDtypeStruct(perturbation.shape...]
    reshape x2 -> x0, local copies, waits for them, and re-layouts: 2.57 us -> none  [the longest x1 1.29 us: on_device(): ln_gain.reshape(1, -1)]
    add x0 -> x1, other arithmetic: none -> 2.06 us  [on_device(): return perturbation * shrink + factor * gradient]
    unnamed x1 -> x2, local copies, waits for them, and re-layouts: 1.98 us -> 0.01 us
where the time goes in v2:
time: 106 us
  Pallas kernels  103 us (97%)
  other arithmetic  2.06 us (2%)
    pallas_call x1, Pallas kernels, on_device(): pl.pallas_call(kernel, out_shape=(jax.ShapeDtypeStruct(perturbation.shape...  103 us

profile of v2, /device:TPU:1, one launch (start us, length us, event | category | flops | bytes accessed | tf_op | source)
XLA Modules:
  0.0 106.2 jit_solution(470452285669039737)
XLA Ops:
  0.0 0.0 copy-start
  0.0 103.2 %shard_map.91 = (f32[4,32,1280]{2,1,0:T(8,128)}, f32[8,128]{1,0:T(8,128)}) custom-call(bf16[4,32,1280]{2,1,0:T(8,128)(2,1)} %pe_in.1, f32[4,32,1280]{2,1,0:T(8,128)} %pert_in.1, bf16[4,32,1280]{2,1,0:T(8,128)(2,1)} %tgt_in.1, f32[1280]{0:T(1024)} %gain_in.1, f32[1280]{0:T(1024)} %bias_in.1, bf16[12,40,1280]{2,1,0:T(8,128)(2,1)} %bitcast.1, ...), custom_call_target="tpu_custom_call" | custom-call | tf_op jit(solution)/shard_map/pallas_call | solution.py:684
  103.2 0.9 slice_reduce_fusion.1
  104.1 0.0 copy-done
  104.1 2.1 %multiply_add_fusion = f32[4,32,1280]{2,1,0:T(8,128)} fusion(f32[4,32,1280]{2,1,0:T(8,128)} %get-tuple-element.8, f32[4,32,1280]{2,1,0:T(8,128)S(1)} %copy-done, f32[4]{0:T(128)S(1)} %get-tuple-element.10, f32[4]{0:T(128)S(1)} %get-tuple-element.9), kind=kLoop, calls=%fused_computation | loop fusion | flops 491520 | bytes 1966112 | tf_op jit(solution)/shard_map/add | solution.py:708
Async XLA Ops:
  0.0 104.1 %copy-start = (f32[4,32,1280]{2,1,0:T(8,128)S(1)}, f32[4,32,1280]{2,1,0:T(8,128)}, u32[]{:S(2)}) copy-start(f32[4,32,1280]{2,1,0:T(8,128)} %pert_in.1) | copy-start | bytes 1966084

commit v3 on v2

--- a/solution.py
+++ b/solution.py
@@ -43,12 +43,12 @@
 
 
 def kernel(
-    pe_in, pert_in, tgt_in, gain_in, bias_in, w_own, wo_own, rad_in, stp_in, grad_out, sums_out,
+    pe_in, pert_in, tgt_in, gain_in, bias_in, w_own, wo_own, rad_in, stp_in, grad_out, shrink_out, factor_out,
     pe, pert, tgt, gain, bias, rad, stp,
     H, RB, Wp, W2, WO, normed, inv, HS, Q, K, V, O, OR, LSE, DOT, GS, GO, GQ, GP, GP2,
     RES, RESB, PF, PB, R1L, R1R, S2L, S2R, R2L, R2R, YS, YR, SC, SCR,
     l_in, l_out, s_rb, r_rb, s_wz, r_wz, s_wy, r_wyl, r_wyr, r_wyy, s_hy, r_hy, s_hx, r_hxl, r_hxr, r_hxy, r_hxz,
-    s_hd, r_hd, s_wo, r_wo, s_woy, r_wol, r_wor, r_woz, s_wod, r_wod, l_wo, s_wd, r_wd, s_oa, r_oa, s_ga, r_ga,
+    s_hd, r_hd, s_wo, r_wo, r_wof, s_woy, r_wol, r_wor, r_woz, s_wod, r_wod, l_wo, s_wd, r_wd, s_oa, r_oa, s_ga, r_ga,
     s_gp, r_gp, s_r1, r_r1l, r_r1r, s_r2, r_r2l, r_r2r, s_ry, r_ry, s_sc, r_sc,
 ):
     s = lax.axis_index("seq")
@@ -80,7 +80,7 @@
     loads = [
         pltpu.make_async_copy(src, dst, l_in.at[i])
         for i, (src, dst) in enumerate(
-            ((pe_in, pe), (pert_in, pert), (tgt_in, tgt), (gain_in, gain), (bias_in, bias),
+            ((pe_in, pe), (pert_in, pert), (gain_in, gain), (bias_in, bias), (tgt_in, tgt),
              (rad_in, rad), (stp_in, stp))
         )
     ]
@@ -89,14 +89,11 @@
 
     barrier = pltpu.get_barrier_semaphore()
 
-    @pl.loop(1, SEQ)
-    def _(d):
+    for d in range(1, SEQ):
         pl.semaphore_signal(
             barrier, inc=1, device_id={"seq": (s + d) % SEQ}, device_id_type=pl.DeviceIdType.MESH
         )
-
-    @pl.loop(1, PLANES)
-    def _(d):
+    for d in range(1, PLANES):
         pl.semaphore_signal(
             barrier, inc=1, device_id={"head": (z + d) % PLANES},
             device_id_type=pl.DeviceIdType.MESH,
@@ -105,27 +102,19 @@
     own_wo = pltpu.make_async_copy(wo_own, WO.at[z, :, pl.ds(0, HD)], l_wo)
     own_wo.start()
 
-    @pl.loop(0, 6)
-    def _(t):
-        Wp[t, HD:PAD, :] = jnp.zeros((PAD - HD, WIDTH), BF16)
-
-    @pl.loop(0, 16)
-    def _(t):
-        WO[t // 2, t % 2, HD:PAD, :] = jnp.zeros((PAD - HD, WIDTH), BF16)
-
-    def layer_norm(image):
+    def normalize(image):
         mixed = pe[image].astype(F32) + pert[image]
         rounded = mixed.astype(BF16).astype(F32)
         center = rounded - jnp.mean(rounded, axis=-1, keepdims=True)
         variance = jnp.mean(center * center, axis=-1, keepdims=True)
         inverse = lax.rsqrt(variance + layer_epsilon)
-        unit = center * inverse
-        normed[image] = unit
-        inv[image] = jnp.broadcast_to(inverse, (BLOCK, PAD))
-        RES[image] = mixed - tgt[image].astype(F32)
+        return mixed, center * inverse, inverse
+
+    def layer_norm(image):
+        _, unit, _ = normalize(image)
         return (unit * gain[...].reshape(1, WIDTH) + bias[...].reshape(1, WIDTH)).astype(BF16)
 
-    for load in loads:
+    for load in loads[:4]:
         load.wait()
 
     @pl.loop(1, ROWS)
@@ -141,6 +130,24 @@
     target = (z + 8 - offset) % 8
 
     half_width = WIDTH // 2
+
+    def ways(plane):
+        odd = plane % 2
+        place = odd * y + (1 - odd) * x
+        return place, odd * down + (1 - odd) * right, odd * up + (1 - odd) * left
+
+    def piece(ref, place, cc):
+        rows = pl.ds(pl.multiple_of(CHUNK * (place % 2), 8), CHUNK)
+        lanes = pl.ds(pl.multiple_of(cc * half_width, PAD), half_width)
+        return ref.at[place // 2, rows, lanes]
+
+    def half_shard(plane, cc):
+        lanes = pl.ds(pl.multiple_of(cc * half_width, PAD), half_width)
+        return WO.at[plane, :, pl.ds(0, HD), lanes]
+
+    place, _, _ = ways(z)
+    for d in (1, 7):
+        send(piece(wo_own, place, c), piece(WO.at[z], place, c), s_wo, r_wo.at[d], head=(z + d) % 8)
 
     def chunk(yy, q):
         u = 3 * yy + q % 3
@@ -214,26 +221,6 @@
         send(chunk(y, j), chunk(y, j), s_wy, r_wyl.at[j], seq=down)
         send(chunk(y, j), chunk(y, j), s_wy, r_wyr.at[j], seq=up)
 
-    def ways(plane):
-        odd = plane % 2
-        place = odd * y + (1 - odd) * x
-        return place, odd * down + (1 - odd) * right, odd * up + (1 - odd) * left
-
-    def piece(ref, place, cc):
-        rows = pl.ds(pl.multiple_of(CHUNK * (place % 2), 8), CHUNK)
-        lanes = pl.ds(pl.multiple_of(cc * half_width, PAD), half_width)
-        return ref.at[place // 2, rows, lanes]
-
-    def half_shard(plane, cc):
-        lanes = pl.ds(pl.multiple_of(cc * half_width, PAD), half_width)
-        return WO.at[plane, :, pl.ds(0, HD), lanes]
-
-    def wo_start():
-        place, _, _ = ways(z)
-        mine, there = piece(wo_own, place, c), piece(WO.at[z], place, c)
-        send(mine, there, s_wo, r_wo.at[1], head=(z + 1) % 8)
-        send(mine, there, s_wo, r_wo.at[7], head=(z + 7) % 8)
-
     def wo_chain(step):
         for d, ahead, there, last in ((step, 1, step + 1, 4), (8 - step, 7, 7 - step, 5)):
             if step == 4 and ahead == 7:
@@ -245,12 +232,31 @@
             if d != last:
                 send(got, got, s_wo, r_wo.at[there], head=(z + ahead) % 8)
 
+    def wo_give():
+        place, _, _ = ways(z)
+        for i, d in enumerate((1, 7)):
+            for part in range(3):
+                spot = (place + 1 + part) % 4
+                send(
+                    piece(wo_own, spot, c), piece(WO.at[z], spot, c), s_wo, r_wof.at[i, part],
+                    head=(z + d) % 8,
+                )
+
+    def wo_near():
+        for i, d in enumerate((1, 7)):
+            plane = (z + 8 - d) % 8
+            place, _, _ = ways(plane)
+            for part in range(3):
+                arrived(piece(WO.at[plane], (place + 1 + part) % 4, c), r_wof.at[i, part])
+            send(half_shard(plane, c), half_shard(plane, c), s_wod, r_wod.at[d], seq=partner)
+
     def wo_first(d):
         plane = (z + 8 - d) % 8
         place, after, before = ways(plane)
         got = piece(WO.at[plane], place, c)
         send(got, got, s_woy, r_wol.at[d], seq=after)
         send(got, got, s_woy, r_wor.at[d], seq=before)
+        send(got, got, s_wod, r_wod.at[d], seq=partner)
 
     def wo_second(d):
         plane = (z + 8 - d) % 8
@@ -259,6 +265,8 @@
         lower, upper = piece(shard, (place + 3) % 4, c), piece(shard, (place + 1) % 4, c)
         arrived(lower, r_wol.at[d])
         arrived(upper, r_wor.at[d])
+        send(lower, lower, s_wod, r_wod.at[d], seq=partner)
+        send(upper, upper, s_wod, r_wod.at[d], seq=partner)
         turn = (plane // 2) % 2
 
         @pl.when(turn == 0)
@@ -272,8 +280,8 @@
     def wo_third(d):
         plane = (z + 8 - d) % 8
         place, _, _ = ways(plane)
-        arrived(piece(WO.at[plane], (place + 2) % 4, c), r_woz.at[d])
-        got = half_shard(plane, c)
+        got = piece(WO.at[plane], (place + 2) % 4, c)
+        arrived(got, r_woz.at[d])
         send(got, got, s_wod, r_wod.at[d], seq=partner)
 
     yu, yd, yo = (y + 3) % 4, (y + 1) % 4, (y + 2) % 4
@@ -293,22 +301,41 @@
         send(H.at[yy, xx, c], H.at[yy, xx, c], s_hd, r_hd.at[d * 4 + 3], seq=partner)
 
     spread(0)
-    wo_start()
+
+    @pl.loop(0, 6)
+    def _(t):
+        Wp[t, HD:PAD, :] = jnp.zeros((PAD - HD, WIDTH), BF16)
+
+    @pl.loop(0, 16)
+    def _(t):
+        WO[t // 2, t % 2, HD:PAD, :] = jnp.zeros((PAD - HD, WIDTH), BF16)
+
+    for load in loads[4:]:
+        load.wait()
+
+    @pl.loop(0, IMAGES)
+    def _(image):
+        mixed, unit, inverse = normalize(image)
+        normed[image] = unit
+        inv[image] = jnp.broadcast_to(inverse, (BLOCK, PAD))
+        RES[image] = mixed - tgt[image].astype(F32)
+
     from_row(1)
     relay(0)
+    wo_chain(1)
     from_row(3)
     pass_on(0)
     pass_on(1)
     from_row(2)
     round_column(0)
     round_column(1)
+    pass_on(3)
+    pass_on(4)
     relay(1)
     round_column(2)
     relay_column(0)
     relay(3)
-    wo_chain(1)
-    pass_on(3)
-    pass_on(4)
+    wo_chain(2)
     relay_column(1)
     relay(2)
     round_column(3)
@@ -316,8 +343,11 @@
     round_column(4)
     far_column(0)
     round_column(5)
+    wo_give()
     relay_column(3)
-    wo_chain(2)
+    wo_chain(3)
+    wo_first(2)
+    wo_first(6)
     far_column(1)
     relay_column(4)
     far_column(3)
@@ -328,8 +358,8 @@
         arrived(chunk(yo, q), r_wyy.at[q])
 
     send(Wp, W2, s_wd, r_wd, seq=partner)
-    wo_chain(3)
-    for d in (1, 7, 2, 6):
+    wo_chain(4)
+    for d in (3, 5, 4):
         wo_first(d)
 
     @pl.loop(0, ROWS)
@@ -339,8 +369,11 @@
         arrived(H.at[yy, (x + 3) % 4, 1 - c], r_hd.at[d * 4 + 1])
         arrived(H.at[yy, (x + 1) % 4, 1 - c], r_hd.at[d * 4 + 2])
         arrived(H.at[yy, (x + 2) % 4, 1 - c], r_hd.at[d * 4 + 3])
-        rows = pl.ds(pl.multiple_of(yy * 256, 256), 256)
-        tokens = H[yy].reshape(256, WIDTH)
+
+    @pl.loop(0, 2)
+    def _(t):
+        rows = pl.ds(pl.multiple_of(t * 512, 512), 512)
+        tokens = H[pl.ds(2 * t, 2)].reshape(512, WIDTH)
         packed = dot(tokens, Wp[...].reshape(6 * PAD, WIDTH), NT).astype(BF16)
         for h in range(2):
             Q[h, rows] = packed[:, (3 * h) * PAD : (3 * h + 1) * PAD]
@@ -348,20 +381,16 @@
             V[h, rows] = packed[:, (3 * h + 2) * PAD : (3 * h + 3) * PAD]
 
     scale = 1.0 / math.sqrt(HD)
-
-    wo_chain(4)
-    for d in (3, 5, 4):
-        wo_first(d)
+    scale2 = scale * math.log2(math.e)
+
+    wo_near()
+    for d in (2, 6):
+        wo_second(d)
 
     @pl.loop(0, 4)
     def _(step):
         row = (y + 3 - step) % 4
 
-        @pl.when(step == 1)
-        def _():
-            for d in (1, 7, 2, 6):
-                wo_second(d)
-
         @pl.when(step == 2)
         def _():
             for d in (3, 5, 4):
@@ -369,30 +398,30 @@
 
         @pl.when(step == 3)
         def _():
-            for d in (1, 7, 2, 6):
+            for d in (2, 6):
                 wo_third(d)
 
         rows = pl.ds(pl.multiple_of(row * TILE, TILE), TILE)
         for h in range(2):
-            scores = dot(Q[h, rows], K[h], NT) * scale
-            top = jnp.max(scores, axis=-1, keepdims=True)
-            grown = jnp.exp(scores - top)
+            scores = dot(Q[h, rows], K[h], NT)
+            top = jnp.max(scores, axis=-1, keepdims=True) * scale2
+            grown = jnp.exp2(scores * scale2 - top)
             total = jnp.sum(grown, axis=-1, keepdims=True)
-            weights = (grown * (1.0 / total)).astype(BF16)
-            part = dot(weights, V[h], NN).astype(BF16)
+            part = (dot(grown.astype(BF16), V[h], NN) * (1.0 / total)).astype(BF16)
             O[h, row] = part.reshape(8, BLOCK, PAD)
-            column = jnp.broadcast_to(top + jnp.log(total), (TILE, PAD))
+            column = jnp.broadcast_to(top + jnp.log2(total), (TILE, PAD))
             LSE[h, :, rows] = jnp.transpose(column)[0:8]
 
-        @pl.loop(0, 8)
-        def _(turn):
-            k = (k8 + 7 - turn) % 8
-            dest = row * 8 + k
-
-            @pl.when(dest != s)
-            def _():
-                for h in range(2):
-                    send(O.at[h, row, k], OR.at[h, y, k8], s_oa, r_oa, seq=dest)
+        def give(turn):
+            k = (k8 + turn) % 8
+            send(O.at[:, row, k], OR.at[:, y, k8], s_oa, r_oa, seq=row * 8 + k)
+
+        for turn in (4, 5, 3, 6, 2, 7, 1):
+            give(turn)
+
+        @pl.when(step != 3)
+        def _():
+            give(0)
 
     for h in range(2):
         OR[h, y, k8] = O[h, y, k8]
@@ -400,15 +429,20 @@
     for d in (3, 5, 4):
         wo_third(d)
     own_wo.wait()
-    for d in range(1, PLANES):
-        arrived(half_shard((z + 8 - d) % 8, 1 - c), r_wod.at[d])
 
     flat_or = OR.reshape(64, BLOCK, PAD)
     arrived(flat_or.at[pl.ds(0, 62)], r_oa)
 
     @pl.loop(0, 8)
-    def _(k):
-        kk = (z + shard_offset((k // 2), k % 2)) % 8
+    def _(turn):
+        k = (turn + 2 * (turn % 2)) % 8
+        away = shard_offset(k // 2, k % 2)
+        kk = (z + away) % 8
+
+        @pl.when(turn != 0)
+        def _():
+            arrived(half_shard(kk, 1 - c), r_wod.at[(8 - away) % 8])
+
         heads = jnp.concatenate([OR[h, :, k].reshape(128, PAD) for h in range(2)], axis=-1)
         branch = dot(heads, WO[kk].reshape(2 * PAD, WIDTH), NN)
         RES[...] += branch.reshape(IMAGES, BLOCK, WIDTH)
@@ -423,15 +457,16 @@
         for h in range(2):
             GS[h, :, k] = back[:, h * PAD : (h + 1) * PAD].reshape(IMAGES, BLOCK, PAD)
 
-        @pl.loop(0, IMAGES)
-        def _(turn):
-            i = (y + 3 - turn) % 4
-            dest = i * 8 + k
-
-            @pl.when(dest != s)
-            def _():
-                for h in range(2):
-                    send(GS.at[h, i, k], GO.at[h, s], s_ga, r_ga, seq=dest)
+        def give(away):
+            i = (y + away) % 4
+            send(GS.at[:, i, k], GO.at[:, s], s_ga, r_ga, seq=i * 8 + k)
+
+        for away in (2, 1, 3):
+            give(away)
+
+        @pl.when(k != k8)
+        def _():
+            give(0)
 
     for h in range(2):
         GO[h, s] = GS[h, y, k8]
@@ -444,6 +479,8 @@
         DOT[h] = jnp.broadcast_to(
             jnp.sum(jnp.transpose(products), axis=0, keepdims=True), (8, 1024)
         )
+
+    GQ[...] = jnp.zeros((2, PAD, 1024), F32)
 
     def store(block_row, h, kind, value):
         parts = value.astype(BF16).reshape(4, 2, BLOCK, PAD)
@@ -457,21 +494,15 @@
         for h in range(2):
             queries = Q[h]
             grads = GO[h].reshape(1024, PAD)
-            scores = dot(K[h, rows], queries, NT) * scale
-            weights = jnp.exp(scores - LSE[h, 0:1])
+            scores = dot(K[h, rows], queries, NT)
+            weights = jnp.exp2(scores * scale2 - LSE[h, 0:1])
             grad_values = dot(weights.astype(BF16), grads, NN)
             grad_weights = dot(V[h, rows], grads, NT)
-            grad_scores = (weights * (grad_weights - DOT[h, 0:1]) * scale).astype(BF16)
-            grad_keys = dot(grad_scores, queries, NN)
-            grad_query = dot(grad_scores, K[h, rows], TN)
-
-            @pl.when(row == 0)
-            def _():
-                GQ[h] = grad_query
-
-            @pl.when(row != 0)
-            def _():
-                GQ[h] += grad_query
+            grad_scores = (weights * (grad_weights - DOT[h, 0:1])).astype(BF16)
+            grad_keys = dot(grad_scores, queries, NN) * scale
+            grad_query = dot(K[h, rows], grad_scores, TN)
+
+            GQ[h] += grad_query
 
             store(row, h, 1, grad_keys)
             store(row, h, 2, grad_values)
@@ -485,7 +516,7 @@
 
     for h in range(2):
         for r in range(4):
-            store(r, h, 0, GQ[h, r * TILE : (r + 1) * TILE])
+            store(r, h, 0, jnp.transpose(GQ[h, :, r * TILE : (r + 1) * TILE]) * scale)
         lanes = pl.ds(h * 3 * PAD, PAD)
         send(GP.at[1 - c, :, :, :, lanes], GP2.at[:, :, :, lanes], s_gp, r_gp.at[h, 4], seq=partner)
 
@@ -497,57 +528,49 @@
 
     xr, xl, xo = (x + 1) % 4, (x + 3) % 4, (x + 2) % 4
 
-    def lanes_of(n):
-        return pl.ds(pl.multiple_of(n * NB, NB), NB)
-
     @pl.loop(0, NSTEPS)
     def _(n):
-        lanes = lanes_of(n)
+        lanes = pl.ds(pl.multiple_of(n * NB, NB), NB)
         mine = GP[c].reshape(512, 6 * PAD)
         other = GP2[...].reshape(512, 6 * PAD)
         part = dot(mine, Wp[:, :, lanes].reshape(6 * PAD, NB), NN)
         part = part + dot(other, W2[:, :, lanes].reshape(6 * PAD, NB), NN)
-        part = part.reshape(4, 4, BLOCK, NB)
-        PF[:, :, :, lanes] = part
-        PB[:, :, lanes] = PF[:, xo, :, lanes].astype(BF16)
-        send(PB.at[:, pl.ds(0, 16), lanes], R1L.at[:, :, lanes], s_r1, r_r1l.at[n], seq=right)
-        send(PB.at[:, pl.ds(16, 16), lanes], R1R.at[:, :, lanes], s_r1, r_r1r.at[n], seq=left)
+        PF[n] = part.reshape(4, 4, BLOCK, NB)
+        PB[n, 0] = PF[n, :, xo, 0:16].astype(BF16)
+        PB[n, 1] = PF[n, :, xo, 16:32].astype(BF16)
+        send(PB.at[n, 0], R1L.at[n], s_r1, r_r1l.at[n], seq=right)
+        send(PB.at[n, 1], R1R.at[n], s_r1, r_r1r.at[n], seq=left)
 
     @pl.loop(0, NSTEPS)
     def _(n):
-        lanes = lanes_of(n)
-        arrived(R1L.at[:, :, lanes], r_r1l.at[n])
-        S2R[:, 0:16, lanes] = (
-            PF[:, xr, 0:16, lanes] + R1L[:, :, lanes].astype(F32)
-        ).astype(BF16)
-        S2R[:, 16:32, lanes] = PF[:, xr, 16:32, lanes].astype(BF16)
-        send(S2R.at[:, :, lanes], R2L.at[:, :, lanes], s_r2, r_r2l.at[n], seq=right)
-        arrived(R1R.at[:, :, lanes], r_r1r.at[n])
-        S2L[:, 16:32, lanes] = (
-            PF[:, xl, 16:32, lanes] + R1R[:, :, lanes].astype(F32)
-        ).astype(BF16)
-        S2L[:, 0:16, lanes] = PF[:, xl, 0:16, lanes].astype(BF16)
-        send(S2L.at[:, :, lanes], R2R.at[:, :, lanes], s_r2, r_r2r.at[n], seq=left)
+        arrived(R1L.at[n], r_r1l.at[n])
+        S2R[n, :, 0:16] = (PF[n, :, xr, 0:16] + R1L[n].astype(F32)).astype(BF16)
+        S2R[n, :, 16:32] = PF[n, :, xr, 16:32].astype(BF16)
+        send(S2R.at[n], R2L.at[n], s_r2, r_r2l.at[n], seq=right)
+        arrived(R1R.at[n], r_r1r.at[n])
+        S2L[n, :, 16:32] = (PF[n, :, xl, 16:32] + R1R[n].astype(F32)).astype(BF16)
+        S2L[n, :, 0:16] = PF[n, :, xl, 0:16].astype(BF16)
+        send(S2L.at[n], R2R.at[n], s_r2, r_r2r.at[n], seq=left)
 
     @pl.loop(0, NSTEPS)
     def _(n):
-        lanes = lanes_of(n)
-        arrived(R2L.at[:, :, lanes], r_r2l.at[n])
-        arrived(R2R.at[:, :, lanes], r_r2r.at[n])
-        total = PF[:, x, :, lanes] + R2L[:, :, lanes].astype(F32) + R2R[:, :, lanes].astype(F32)
-        YS[:, :, lanes] = total.astype(BF16)
-        for d in range(1, 4):
+        arrived(R2L.at[n], r_r2l.at[n])
+        arrived(R2R.at[n], r_r2r.at[n])
+        total = PF[n, :, x] + R2L[n].astype(F32) + R2R[n].astype(F32)
+        YS[n] = total.astype(BF16)
+        for d in (2, 1, 3):
             send(
-                YS.at[(y + d) % 4, :, lanes], YR.at[y, :, lanes], s_ry, r_ry.at[d - 1, n],
+                YS.at[n, (y + d) % 4], YR.at[y, n], s_ry, r_ry.at[d - 1, n],
                 seq=at((y + d) % 4, x, c),
             )
 
-    YR[y] = YS[y]
+    for n in range(NSTEPS):
+        YR[y, n] = YS[n, y]
 
     @pl.loop(0, NSTEPS)
     def _(n):
         for d in range(1, 4):
-            arrived(YR.at[(y + d) % 4, :, lanes_of(n)], r_ry.at[3 - d, n])
+            arrived(YR.at[(y + d) % 4, n], r_ry.at[3 - d, n])
 
     lane = lax.broadcasted_iota(jnp.int32, (8, PAD), 1)
     line = lax.broadcasted_iota(jnp.int32, (8, PAD), 0)
@@ -557,7 +580,8 @@
 
     sums = jnp.zeros((8, PAD), F32)
     for i in range(IMAGES):
-        scaled = YR[i].astype(F32) * gain[...].reshape(1, WIDTH)
+        back = jnp.concatenate([YR[i, n] for n in range(NSTEPS)], axis=-1)
+        scaled = back.astype(F32) * gain[...].reshape(1, WIDTH)
         unit = normed[i]
         first = jnp.mean(scaled, axis=-1, keepdims=True)
         second = jnp.mean(scaled * unit, axis=-1, keepdims=True)
@@ -570,8 +594,7 @@
     SC[...] = sums
     SCR[s] = sums
 
-    @pl.loop(1, SEQ)
-    def _(d):
+    for d in (18, 20, 22, 16, 17, 19, 21, 23, *range(8, 16), *range(24, 32), *range(1, 8)):
         send(SC, SCR.at[s], s_sc, r_sc, seq=(s + d) % SEQ)
 
     arrived(SCR.at[pl.ds(0, SEQ - 1)], r_sc)
@@ -585,7 +608,12 @@
     factor = step_of / jnp.sqrt(grad_square + norm_epsilon)
     stepped_square = own + 2.0 * factor * cross + factor * factor * grad_square
     shrink = jnp.minimum(1.0, radius_of / jnp.sqrt(stepped_square + norm_epsilon))
-    sums_out[...] = jnp.where(lane == 0, shrink, factor * shrink)
+    shrink_row, factor_row = jnp.zeros((1, PAD), F32), jnp.zeros((1, PAD), F32)
+    for i in range(IMAGES):
+        shrink_row = jnp.where(lane[0:1] == i, shrink[i : i + 1], shrink_row)
+        factor_row = jnp.where(lane[0:1] == i, (factor * shrink)[i : i + 1], factor_row)
+    shrink_out[...] = shrink_row.reshape(PAD)
+    factor_out[...] = factor_row.reshape(PAD)
     for i in range(IMAGES):
         pltpu.make_async_copy(RES.at[i], grad_out.at[i], l_out.at[i]).wait()
 
@@ -608,8 +636,12 @@
     arrived(Wp, s_wd)
     for d in range(1, PLANES):
         arrived(piece(wo_own, y, c), s_wo)
-        for _ in range(3):
-            arrived(piece(wo_own, y, c), s_woy)
+        if d in (1, 7):
+            for _ in range(3):
+                arrived(piece(wo_own, y, c), s_wo)
+        else:
+            for _ in range(3):
+                arrived(piece(wo_own, y, c), s_woy)
         arrived(half_shard(z, c), s_wod)
     arrived(flat_or.at[pl.ds(0, 62)], s_oa)
     arrived(flat_go.at[pl.ds(0, 62)], s_ga)
@@ -617,7 +649,8 @@
     arrived(PB, s_r1)
     arrived(S2R, s_r2)
     arrived(S2L, s_r2)
-    arrived(YS.at[pl.ds(0, 3)], s_ry)
+    for _ in range(3):
+        arrived(YR.at[pl.ds(0, 1)], s_ry)
     arrived(SCR.at[pl.ds(0, SEQ - 1)], s_sc)
 
 
@@ -651,28 +684,28 @@
         V((2, 8, 1024), F32),
         V((2, 4, 8, BLOCK, PAD), BF16),
         V((2, 32, BLOCK, PAD), BF16),
-        V((2, 1024, PAD), F32),
+        V((2, PAD, 1024), F32),
         V((2, 4, 4, BLOCK, 6 * PAD), BF16),
         V((4, 4, BLOCK, 6 * PAD), BF16),
         V((IMAGES, BLOCK, WIDTH), F32),
         V((IMAGES * BLOCK, WIDTH), BF16),
-        V((4, 4, BLOCK, WIDTH), F32),
-        V((4, BLOCK, WIDTH), BF16),
-        V((4, 16, WIDTH), BF16),
-        V((4, 16, WIDTH), BF16),
-        V((4, BLOCK, WIDTH), BF16),
-        V((4, BLOCK, WIDTH), BF16),
-        V((4, BLOCK, WIDTH), BF16),
-        V((4, BLOCK, WIDTH), BF16),
-        V((4, BLOCK, WIDTH), BF16),
-        V((4, BLOCK, WIDTH), BF16),
+        V((NSTEPS, 4, 4, BLOCK, NB), F32),
+        V((NSTEPS, 2, 4, 16, NB), BF16),
+        V((NSTEPS, 4, 16, NB), BF16),
+        V((NSTEPS, 4, 16, NB), BF16),
+        V((NSTEPS, 4, BLOCK, NB), BF16),
+        V((NSTEPS, 4, BLOCK, NB), BF16),
+        V((NSTEPS, 4, BLOCK, NB), BF16),
+        V((NSTEPS, 4, BLOCK, NB), BF16),
+        V((NSTEPS, 4, BLOCK, NB), BF16),
+        V((4, NSTEPS, BLOCK, NB), BF16),
         V((8, PAD), F32),
         V((SEQ, 8, PAD), F32),
         dma((7,)), dma((IMAGES,)), dma, dma((4,)),
         dma, dma((CHUNKS,)), dma, dma((CHUNKS,)), dma((CHUNKS,)), dma((CHUNKS,)),
         dma, dma((3,)), dma, dma((4,)), dma((4,)), dma((4,)), dma((4,)),
         dma, dma((16,)),
-        dma, dma((8,)), dma, dma((8,)), dma((8,)), dma((8,)), dma, dma((8,)), dma,
+        dma, dma((8,)), dma((2, 3)), dma, dma((8,)), dma((8,)), dma((8,)), dma, dma((8,)), dma,
         dma, dma,
         dma, dma, dma, dma,
         dma, dma((2, 5)),
@@ -681,14 +714,15 @@
         dma, dma((3, NSTEPS)),
         dma, dma,
     ]
-    gradient, sums = pl.pallas_call(
+    gradient, shrink, factor = pl.pallas_call(
         kernel,
         out_shape=(
             jax.ShapeDtypeStruct(perturbation.shape, F32),
-            jax.ShapeDtypeStruct((8, PAD), F32),
+            jax.ShapeDtypeStruct((PAD,), F32),
+            jax.ShapeDtypeStruct((PAD,), F32),
         ),
         in_specs=[anywhere] * 9,
-        out_specs=(anywhere, vmem),
+        out_specs=(anywhere, vmem, vmem),
         scratch_shapes=scratch,
         compiler_params=pltpu.CompilerParams(
             collective_id=0, has_side_effects=True, vmem_limit_bytes=62 * 1024 * 1024
@@ -704,8 +738,7 @@
         radius,
         step_size,
     )
-    shrink, factor = sums[:IMAGES, 0:1, None], sums[:IMAGES, 1:2, None]
-    return perturbation * shrink + factor * gradient
+    return perturbation * shrink[:IMAGES, None, None] + factor[:IMAGES, None, None] * gradient
 
 
 def solution(mesh):

time: 106 us -> 96.1 us (0.907)
  Pallas kernels: 103 us -> 93.9 us
    pallas_call x1, Pallas kernels: 103 us -> 93.9 us  [on_device(): pl.pallas_call(kernel, out_shape=(jax.ShapeDtypeStruct(perturbation.shape...]
where the time goes in v3:
time: 96.1 us; the launch traced here: 96 us
  Pallas kernels  93.9 us (98%)
  other arithmetic  2.07 us (2%)
    pallas_call x1, Pallas kernels, on_device(): pl.pallas_call(kernel, out_shape=(jax.ShapeDtypeStruct(perturbation.shape...  93.9 us
    add x1, other arithmetic, on_device(): perturbation * shrink[:IMAGES, None, None]  2.07 us

profile of v3, /device:TPU:1, one launch (start us, length us, event | category | flops | bytes accessed | tf_op | source)
XLA Modules:
  0.0 96.0 jit_solution(8485034128848948455)
XLA Ops:
  0.0 0.0 copy-start
  0.0 93.9 %shard_map.91 = (f32[4,32,1280]{2,1,0:T(8,128)}, f32[128]{0:T(128)}, f32[128]{0:T(128)}) custom-call(bf16[4,32,1280]{2,1,0:T(8,128)(2,1)} %pe_in.1, f32[4,32,1280]{2,1,0:T(8,128)} %pert_in.1, bf16[4,32,1280]{2,1,0:T(8,128)(2,1)} %tgt_in.1, f32[1280]{0:T(1024)} %gain_in.1, f32[1280]{0:T(1024)} %bias_in.1, bf16[12,40,1280]{2,1,0:T(8,128)(2,1)} %bitcast.3, ...), custom_call_target="tpu_custom_call" | custom-call | tf_op jit(solution)/shard_map/pallas_call | solution.py:717
  93.9 0.0 copy-done
  93.9 2.1 %multiply_add_fusion = f32[4,32,1280]{2,1,0:T(8,128)} fusion(f32[4,32,1280]{2,1,0:T(8,128)} %get-tuple-element.10, f32[4,32,1280]{2,1,0:T(8,128)S(1)} %copy-done, f32[4]{0:T(128)} %bitcast.5, f32[4]{0:T(128)} %bitcast.4), kind=kLoop, calls=%fused_computation | loop fusion | flops 491520 | bytes 1966112 | tf_op jit(solution)/shard_map/add | solution.py:741
Async XLA Ops:
  0.0 93.9 %copy-start = (f32[4,32,1280]{2,1,0:T(8,128)S(1)}, f32[4,32,1280]{2,1,0:T(8,128)}, u32[]{:S(2)}) copy-start(f32[4,32,1280]{2,1,0:T(8,128)} %pert_in.1) | copy-start | bytes 1966084

commit v4 on v3

--- a/solution.py
+++ b/solution.py
@@ -25,6 +25,7 @@
 BLOCK = 32
 WIDTH = 1280
 HD = 80
+PACKED = 40
 PAD = 128
 CHUNK = 40
 NB = 256
@@ -37,6 +38,28 @@
     return lax.dot_general(a, b, dims, preferred_element_type=F32)
 
 
+def lane_of(value):
+    return lax.broadcasted_iota(jnp.int32, value.shape, value.ndim - 1)
+
+
+def pack_rest(rest):
+    groups = rest.reshape(-1, 4, 8, PAD)
+    packed = groups[:, 0].reshape(-1, PAD)
+    lane = lane_of(packed)
+    for g in range(1, 4):
+        turned = pltpu.roll(groups[:, g].reshape(-1, PAD), 32 * g, 1)
+        packed = jnp.where(lane >= 32 * g, turned, packed)
+    return packed.reshape(-1, 8, PAD)
+
+
+def unpack_rest(packed, lane):
+    flat = packed.reshape(-1, PAD)
+    groups = [
+        pltpu.roll(flat, (PAD + lane - 32 * g) % PAD, 1).reshape(-1, 1, 8, PAD) for g in range(4)
+    ]
+    return jnp.concatenate(groups, axis=1).reshape(-1, PAD)
+
+
 def shard_offset(x, c):
     other = 8 - x - 4 * (1 - (x + 3) // 4)
     return (1 - c) * x + c * other
@@ -45,9 +68,9 @@
 def kernel(
     pe_in, pert_in, tgt_in, gain_in, bias_in, w_own, wo_own, rad_in, stp_in, grad_out, shrink_out, factor_out,
     pe, pert, tgt, gain, bias, rad, stp,
-    H, RB, Wp, W2, WO, normed, inv, HS, Q, K, V, O, OR, LSE, DOT, GS, GO, GQ, GP, GP2,
-    RES, RESB, PF, PB, R1L, R1R, S2L, S2R, R2L, R2R, YS, YR, SC, SCR,
-    l_in, l_out, s_rb, r_rb, s_wz, r_wz, s_wy, r_wyl, r_wyr, r_wyy, s_hy, r_hy, s_hx, r_hxl, r_hxr, r_hxy, r_hxz,
+    H, RB, Wp, W2, WO, normed, inv, HS, Q, K, V, O, OS, OR, LSE, DOT, GS, GO, GH, GQ, GP, GP2,
+    RES, RESB, PF, PB, R1L, R1R, S2L, S2R, R2L, R2R, YS, YR, SC, SCR, SHRINK, FACTOR,
+    l_in, l_out, l_res, s_rb, r_rb, s_wz, r_wz, s_wy, r_wyl, r_wyr, r_wyy, s_hy, r_hy, s_hx, r_hxl, r_hxr, r_hxy, r_hxz,
     s_hd, r_hd, s_wo, r_wo, r_wof, s_woy, r_wol, r_wor, r_woz, s_wod, r_wod, l_wo, s_wd, r_wd, s_oa, r_oa, s_ga, r_ga,
     s_gp, r_gp, s_r1, r_r1l, r_r1r, s_r2, r_r2l, r_r2r, s_ry, r_ry, s_sc, r_sc,
 ):
@@ -99,7 +122,7 @@
             device_id_type=pl.DeviceIdType.MESH,
         )
 
-    own_wo = pltpu.make_async_copy(wo_own, WO.at[z, :, pl.ds(0, HD)], l_wo)
+    own_wo = pltpu.make_async_copy(wo_own, WO.at[z, pl.ds(0, 2 * HD)], l_wo)
     own_wo.start()
 
     def normalize(image):
@@ -137,13 +160,13 @@
         return place, odd * down + (1 - odd) * right, odd * up + (1 - odd) * left
 
     def piece(ref, place, cc):
-        rows = pl.ds(pl.multiple_of(CHUNK * (place % 2), 8), CHUNK)
+        rows = pl.ds(pl.multiple_of(CHUNK * place, 8), CHUNK)
         lanes = pl.ds(pl.multiple_of(cc * half_width, PAD), half_width)
-        return ref.at[place // 2, rows, lanes]
+        return ref.at[rows, lanes]
 
     def half_shard(plane, cc):
         lanes = pl.ds(pl.multiple_of(cc * half_width, PAD), half_width)
-        return WO.at[plane, :, pl.ds(0, HD), lanes]
+        return WO.at[plane, pl.ds(0, 2 * HD), lanes]
 
     place, _, _ = ways(z)
     for d in (1, 7):
@@ -306,9 +329,9 @@
     def _(t):
         Wp[t, HD:PAD, :] = jnp.zeros((PAD - HD, WIDTH), BF16)
 
-    @pl.loop(0, 16)
+    @pl.loop(0, PLANES)
     def _(t):
-        WO[t // 2, t % 2, HD:PAD, :] = jnp.zeros((PAD - HD, WIDTH), BF16)
+        WO[t, 2 * HD : 2 * PAD, :] = jnp.zeros((2 * (PAD - HD), WIDTH), BF16)
 
     for load in loads[4:]:
         load.wait()
@@ -402,19 +425,26 @@
                 wo_third(d)
 
         rows = pl.ds(pl.multiple_of(row * TILE, TILE), TILE)
+        parts = []
         for h in range(2):
             scores = dot(Q[h, rows], K[h], NT)
             top = jnp.max(scores, axis=-1, keepdims=True) * scale2
             grown = jnp.exp2(scores * scale2 - top)
             total = jnp.sum(grown, axis=-1, keepdims=True)
-            part = (dot(grown.astype(BF16), V[h], NN) * (1.0 / total)).astype(BF16)
-            O[h, row] = part.reshape(8, BLOCK, PAD)
+            part = dot(grown.astype(BF16), V[h], NN) * (1.0 / total)
+            parts.append(part)
+            O[h, row] = part.astype(BF16).reshape(8, BLOCK, PAD)
             column = jnp.broadcast_to(top + jnp.log2(total), (TILE, PAD))
             LSE[h, :, rows] = jnp.transpose(column)[0:8]
 
+        turned = pltpu.roll(parts[1], HD, 1)
+        whole = jnp.where(lane_of(turned) < HD, parts[0], turned)
+        OS[row, :, 0:BLOCK] = whole.astype(BF16).reshape(8, BLOCK, PAD)
+        OS[row, :, BLOCK:PACKED] = pack_rest(turned).astype(BF16)
+
         def give(turn):
             k = (k8 + turn) % 8
-            send(O.at[:, row, k], OR.at[:, y, k8], s_oa, r_oa, seq=row * 8 + k)
+            send(OS.at[row, k], OR.at[s], s_oa, r_oa, seq=row * 8 + k)
 
         for turn in (4, 5, 3, 6, 2, 7, 1):
             give(turn)
@@ -423,15 +453,13 @@
         def _():
             give(0)
 
-    for h in range(2):
-        OR[h, y, k8] = O[h, y, k8]
+    OR[s] = OS[y, k8]
 
     for d in (3, 5, 4):
         wo_third(d)
     own_wo.wait()
 
-    flat_or = OR.reshape(64, BLOCK, PAD)
-    arrived(flat_or.at[pl.ds(0, 62)], r_oa)
+    arrived(OR.at[pl.ds(0, SEQ - 1)], r_oa)
 
     @pl.loop(0, 8)
     def _(turn):
@@ -443,8 +471,12 @@
         def _():
             arrived(half_shard(kk, 1 - c), r_wod.at[(8 - away) % 8])
 
-        heads = jnp.concatenate([OR[h, :, k].reshape(128, PAD) for h in range(2)], axis=-1)
-        branch = dot(heads, WO[kk].reshape(2 * PAD, WIDTH), NN)
+        rest = jnp.concatenate([OR[i * 8 + k, BLOCK:PACKED] for i in range(IMAGES)], axis=0)
+        rest = unpack_rest(rest.astype(F32), 0)
+        rest = jnp.where(lane_of(rest) < 32, rest, 0.0).astype(BF16)
+        whole = jnp.concatenate([OR[i * 8 + k, 0:BLOCK] for i in range(IMAGES)], axis=0)
+        heads = jnp.concatenate([whole, rest], axis=-1)
+        branch = dot(heads, WO[kk], NN)
         RES[...] += branch.reshape(IMAGES, BLOCK, WIDTH)
 
     RESB[...] = RES[...].reshape(128, WIDTH).astype(BF16)
@@ -453,13 +485,13 @@
     def _(turn):
         k = ((x + 3 - turn // 2) % 4) * 2 + turn % 2
         kk = (z + shard_offset((k // 2), k % 2)) % 8
-        back = dot(RESB[...], WO[kk].reshape(2 * PAD, WIDTH), NT).astype(BF16)
-        for h in range(2):
-            GS[h, :, k] = back[:, h * PAD : (h + 1) * PAD].reshape(IMAGES, BLOCK, PAD)
+        back = dot(RESB[...], WO[kk], NT)
+        GS[:, k, 0:BLOCK] = back[:, 0:PAD].astype(BF16).reshape(IMAGES, BLOCK, PAD)
+        GS[:, k, BLOCK:PACKED] = pack_rest(back[:, PAD : 2 * PAD]).astype(BF16)
 
         def give(away):
             i = (y + away) % 4
-            send(GS.at[:, i, k], GO.at[:, s], s_ga, r_ga, seq=i * 8 + k)
+            send(GS.at[i, k], GO.at[s], s_ga, r_ga, seq=i * 8 + k)
 
         for away in (2, 1, 3):
             give(away)
@@ -468,14 +500,25 @@
         def _():
             give(0)
 
+    GO[s] = GS[y, k8]
+
+    arrived(GO.at[pl.ds(0, SEQ - 1)], r_ga)
+
+    @pl.loop(0, 4)
+    def _(row):
+        blocks = pl.ds(row * 8, 8)
+        rows = pl.ds(pl.multiple_of(row * TILE, TILE), TILE)
+        whole = GO[blocks, 0:BLOCK].astype(F32).reshape(TILE, PAD)
+        rest = unpack_rest(GO[blocks, BLOCK:PACKED].astype(F32), PAD - HD)
+        lane = lane_of(whole)
+        turned = pltpu.roll(whole, PAD - HD, 1)
+        GH[0, rows] = jnp.where(lane < HD, whole, 0.0).astype(BF16)
+        GH[1, rows] = jnp.where(
+            lane < PAD - HD, turned, jnp.where(lane < HD, rest, 0.0)
+        ).astype(BF16)
+
     for h in range(2):
-        GO[h, s] = GS[h, y, k8]
-
-    flat_go = GO.reshape(64, BLOCK, PAD)
-    arrived(flat_go.at[pl.ds(0, 62)], r_ga)
-
-    for h in range(2):
-        products = GO[h].reshape(1024, PAD).astype(F32) * O[h].reshape(1024, PAD).astype(F32)
+        products = GH[h].astype(F32) * O[h].reshape(1024, PAD).astype(F32)
         DOT[h] = jnp.broadcast_to(
             jnp.sum(jnp.transpose(products), axis=0, keepdims=True), (8, 1024)
         )
@@ -493,7 +536,7 @@
         rows = pl.ds(pl.multiple_of(row * TILE, TILE), TILE)
         for h in range(2):
             queries = Q[h]
-            grads = GO[h].reshape(1024, PAD)
+            grads = GH[h]
             scores = dot(K[h, rows], queries, NT)
             weights = jnp.exp2(scores * scale2 - LSE[h, 0:1])
             grad_values = dot(weights.astype(BF16), grads, NN)
@@ -612,8 +655,14 @@
     for i in range(IMAGES):
         shrink_row = jnp.where(lane[0:1] == i, shrink[i : i + 1], shrink_row)
         factor_row = jnp.where(lane[0:1] == i, (factor * shrink)[i : i + 1], factor_row)
-    shrink_out[...] = shrink_row.reshape(PAD)
-    factor_out[...] = factor_row.reshape(PAD)
+    SHRINK[...] = shrink_row.reshape(PAD)
+    FACTOR[...] = factor_row.reshape(PAD)
+    results = [
+        pltpu.make_async_copy(SHRINK, shrink_out, l_res.at[0]),
+        pltpu.make_async_copy(FACTOR, factor_out, l_res.at[1]),
+    ]
+    for result in results:
+        result.start()
     for i in range(IMAGES):
         pltpu.make_async_copy(RES.at[i], grad_out.at[i], l_out.at[i]).wait()
 
@@ -643,8 +692,8 @@
             for _ in range(3):
                 arrived(piece(wo_own, y, c), s_woy)
         arrived(half_shard(z, c), s_wod)
-    arrived(flat_or.at[pl.ds(0, 62)], s_oa)
-    arrived(flat_go.at[pl.ds(0, 62)], s_ga)
+    arrived(OR.at[pl.ds(0, SEQ - 1)], s_oa)
+    arrived(GO.at[pl.ds(0, SEQ - 1)], s_ga)
     arrived(GP2, s_gp)
     arrived(PB, s_r1)
     arrived(S2R, s_r2)
@@ -652,10 +701,11 @@
     for _ in range(3):
         arrived(YR.at[pl.ds(0, 1)], s_ry)
     arrived(SCR.at[pl.ds(0, SEQ - 1)], s_sc)
+    for result in results:
+        result.wait()
 
 
 def on_device(patch_embed, perturbation, target, ln_gain, ln_bias, w_qkv, w_out, radius, step_size):
-    vmem = pl.BlockSpec(memory_space=pltpu.VMEM)
     anywhere = pl.BlockSpec(memory_space=pl.ANY)
     dma = pltpu.SemaphoreType.DMA
     V = pltpu.VMEM
@@ -671,7 +721,7 @@
         V((4, CHUNK, WIDTH // 2), BF16),
         V((6, PAD, WIDTH), BF16),
         V((6, PAD, WIDTH), BF16),
-        V((PLANES, 2, PAD, WIDTH), BF16),
+        V((PLANES, 2 * PAD, WIDTH), BF16),
         V((IMAGES, BLOCK, WIDTH), F32),
         V((IMAGES, BLOCK, PAD), F32),
         V((IMAGES, BLOCK, WIDTH), BF16),
@@ -679,11 +729,13 @@
         V((2, 1024, PAD), BF16),
         V((2, 1024, PAD), BF16),
         V((2, 4, 8, BLOCK, PAD), BF16),
-        V((2, 4, 8, BLOCK, PAD), BF16),
+        V((4, 8, PACKED, PAD), BF16),
+        V((SEQ, PACKED, PAD), BF16),
         V((2, 8, 1024), F32),
         V((2, 8, 1024), F32),
-        V((2, 4, 8, BLOCK, PAD), BF16),
-        V((2, 32, BLOCK, PAD), BF16),
+        V((4, 8, PACKED, PAD), BF16),
+        V((32, PACKED, PAD), BF16),
+        V((2, 1024, PAD), BF16),
         V((2, PAD, 1024), F32),
         V((2, 4, 4, BLOCK, 6 * PAD), BF16),
         V((4, 4, BLOCK, 6 * PAD), BF16),
@@ -701,7 +753,9 @@
         V((4, NSTEPS, BLOCK, NB), BF16),
         V((8, PAD), F32),
         V((SEQ, 8, PAD), F32),
-        dma((7,)), dma((IMAGES,)), dma, dma((4,)),
+        V((PAD,), F32),
+        V((PAD,), F32),
+        dma((7,)), dma((IMAGES,)), dma((2,)), dma, dma((4,)),
         dma, dma((CHUNKS,)), dma, dma((CHUNKS,)), dma((CHUNKS,)), dma((CHUNKS,)),
         dma, dma((3,)), dma, dma((4,)), dma((4,)), dma((4,)), dma((4,)),
         dma, dma((16,)),
@@ -722,7 +776,7 @@
             jax.ShapeDtypeStruct((PAD,), F32),
         ),
         in_specs=[anywhere] * 9,
-        out_specs=(anywhere, vmem, vmem),
+        out_specs=(anywhere,) * 3,
         scratch_shapes=scratch,
         compiler_params=pltpu.CompilerParams(
             collective_id=0, has_side_effects=True, vmem_limit_bytes=62 * 1024 * 1024
@@ -734,7 +788,7 @@
         ln_gain,
         ln_bias,
         w_qkv.reshape(12, CHUNK, WIDTH),
-        w_out,
+        w_out.reshape(2 * HD, WIDTH),
         radius,
         step_size,
     )

time: 96.1 us -> 93.9 us (0.977)
  Pallas kernels: 93.9 us -> 91.7 us
    pallas_call x1, Pallas kernels: 93.9 us -> 91.7 us  [on_device(): pl.pallas_call(kernel, out_shape=(jax.ShapeDtypeStruct(perturbation.shape...]
where the time goes in v4:
time: 93.9 us; the launch traced here: 93.8 us
  Pallas kernels  91.7 us (98%)
  other arithmetic  2.07 us (2%)
    pallas_call x1, Pallas kernels, on_device(): pl.pallas_call(kernel, out_shape=(jax.ShapeDtypeStruct(perturbation.shape...  91.7 us
    add x1, other arithmetic, on_device(): perturbation * shrink[:IMAGES, None, None]  2.07 us

profile of v4, /device:TPU:1, one launch (start us, length us, event | category | flops | bytes accessed | tf_op | source)
XLA Modules:
  0.0 93.8 jit_solution(17419961574068383733)
XLA Ops:
  0.0 0.0 copy-start
  0.0 91.7 %shard_map.91 = (f32[4,32,1280]{2,1,0:T(8,128)}, f32[128]{0:T(128)}, f32[128]{0:T(128)}) custom-call(bf16[4,32,1280]{2,1,0:T(8,128)(2,1)} %pe_in.1, f32[4,32,1280]{2,1,0:T(8,128)} %pert_in.1, bf16[4,32,1280]{2,1,0:T(8,128)(2,1)} %tgt_in.1, f32[1280]{0:T(1024)} %gain_in.1, f32[1280]{0:T(1024)} %bias_in.1, bf16[12,40,1280]{2,1,0:T(8,128)(2,1)} %bitcast.4, ...), custom_call_target="tpu_custom_call" | custom-call | tf_op jit(solution)/shard_map/pallas_call | solution.py:771
  91.7 0.0 copy-done
  91.7 2.1 %multiply_add_fusion = f32[4,32,1280]{2,1,0:T(8,128)} fusion(f32[4,32,1280]{2,1,0:T(8,128)} %get-tuple-element.10, f32[4,32,1280]{2,1,0:T(8,128)S(1)} %copy-done, f32[4]{0:T(128)} %bitcast.7, f32[4]{0:T(128)} %bitcast.6), kind=kLoop, calls=%fused_computation | loop fusion | flops 491520 | bytes 1966112 | tf_op jit(solution)/shard_map/add | solution.py:795
Async XLA Ops:
  0.0 91.7 %copy-start = (f32[4,32,1280]{2,1,0:T(8,128)S(1)}, f32[4,32,1280]{2,1,0:T(8,128)}, u32[]{:S(2)}) copy-start(f32[4,32,1280]{2,1,0:T(8,128)} %pert_in.1) | copy-start | bytes 1966084

commit v5 on v4

--- a/solution.py
+++ b/solution.py
@@ -414,15 +414,10 @@
     def _(step):
         row = (y + 3 - step) % 4
 
-        @pl.when(step == 2)
+        @pl.when(step == 3)
         def _():
             for d in (3, 5, 4):
                 wo_second(d)
-
-        @pl.when(step == 3)
-        def _():
-            for d in (2, 6):
-                wo_third(d)
 
         rows = pl.ds(pl.multiple_of(row * TILE, TILE), TILE)
         parts = []
@@ -455,50 +450,54 @@
 
     OR[s] = OS[y, k8]
 
-    for d in (3, 5, 4):
+    for d in (2, 6, 3, 5, 4):
         wo_third(d)
     own_wo.wait()
 
     arrived(OR.at[pl.ds(0, SEQ - 1)], r_oa)
 
-    @pl.loop(0, 8)
+    @pl.loop(0, 4)
     def _(turn):
-        k = (turn + 2 * (turn % 2)) % 8
-        away = shard_offset(k // 2, k % 2)
-        kk = (z + away) % 8
-
-        @pl.when(turn != 0)
-        def _():
-            arrived(half_shard(kk, 1 - c), r_wod.at[(8 - away) % 8])
-
-        rest = jnp.concatenate([OR[i * 8 + k, BLOCK:PACKED] for i in range(IMAGES)], axis=0)
-        rest = unpack_rest(rest.astype(F32), 0)
-        rest = jnp.where(lane_of(rest) < 32, rest, 0.0).astype(BF16)
-        whole = jnp.concatenate([OR[i * 8 + k, 0:BLOCK] for i in range(IMAGES)], axis=0)
-        heads = jnp.concatenate([whole, rest], axis=-1)
-        branch = dot(heads, WO[kk], NN)
+        pair = [(k, shard_offset(k // 2, k % 2)) for k in (2 * turn, (2 * turn + 3) % 8)]
+        for _, away in pair:
+            @pl.when(away != 0)
+            def _(away=away):
+                arrived(half_shard((z + away) % 8, 1 - c), r_wod.at[(8 - away) % 8])
+
+        branch = jnp.zeros((128, WIDTH), F32)
+        for k, away in pair:
+            rest = jnp.concatenate([OR[i * 8 + k, BLOCK:PACKED] for i in range(IMAGES)], axis=0)
+            rest = unpack_rest(rest.astype(F32), 0)
+            rest = jnp.where(lane_of(rest) < 32, rest, 0.0).astype(BF16)
+            whole = jnp.concatenate([OR[i * 8 + k, 0:BLOCK] for i in range(IMAGES)], axis=0)
+            heads = jnp.concatenate([whole, rest], axis=-1)
+            branch = branch + dot(heads, WO[(z + away) % 8], NN)
         RES[...] += branch.reshape(IMAGES, BLOCK, WIDTH)
 
     RESB[...] = RES[...].reshape(128, WIDTH).astype(BF16)
 
-    @pl.loop(0, 8)
+    @pl.loop(0, 4)
     def _(turn):
-        k = ((x + 3 - turn // 2) % 4) * 2 + turn % 2
-        kk = (z + shard_offset((k // 2), k % 2)) % 8
-        back = dot(RESB[...], WO[kk], NT)
-        GS[:, k, 0:BLOCK] = back[:, 0:PAD].astype(BF16).reshape(IMAGES, BLOCK, PAD)
-        GS[:, k, BLOCK:PACKED] = pack_rest(back[:, PAD : 2 * PAD]).astype(BF16)
-
-        def give(away):
-            i = (y + away) % 4
+        xx = (x + 3 - turn) % 4
+        for cc in range(2):
+            back = dot(RESB[...], WO[(z + shard_offset(xx, cc)) % 8], NT)
+            GS[:, 2 * xx + cc, 0:BLOCK] = (
+                back[:, 0:PAD].astype(BF16).reshape(IMAGES, BLOCK, PAD)
+            )
+            GS[:, 2 * xx + cc, BLOCK:PACKED] = pack_rest(back[:, PAD : 2 * PAD]).astype(BF16)
+
+        def give(away, cc):
+            i, k = (y + away) % 4, 2 * xx + cc
             send(GS.at[i, k], GO.at[s], s_ga, r_ga, seq=i * 8 + k)
 
         for away in (2, 1, 3):
-            give(away)
-
-        @pl.when(k != k8)
-        def _():
-            give(0)
+            for cc in range(2):
+                give(away, cc)
+
+        for cc in range(2):
+            @pl.when(2 * xx + cc != k8)
+            def _(cc=cc):
+                give(0, cc)
 
     GO[s] = GS[y, k8]
 

time: 93.9 us -> 92.6 us (0.986)
  Pallas kernels: 91.7 us -> 90.4 us
    pallas_call x1, Pallas kernels: 91.7 us -> 90.4 us  [on_device(): pl.pallas_call(kernel, out_shape=(jax.ShapeDtypeStruct(perturbation.shape...]
where the time goes in v5:
time: 92.6 us; the launch traced here: 92.5 us
  Pallas kernels  90.4 us (98%)
  other arithmetic  2.07 us (2%)
    pallas_call x1, Pallas kernels, on_device(): pl.pallas_call(kernel, out_shape=(jax.ShapeDtypeStruct(perturbation.shape...  90.4 us
    add x1, other arithmetic, on_device(): perturbation * shrink[:IMAGES, None, None]  2.07 us

profile of v5, /device:TPU:1, one launch (start us, length us, event | category | flops | bytes accessed | tf_op | source)
XLA Modules:
  0.0 92.5 jit_solution(14394460552921142563)
XLA Ops:
  0.0 0.0 copy-start
  0.0 90.4 %shard_map.91 = (f32[4,32,1280]{2,1,0:T(8,128)}, f32[128]{0:T(128)}, f32[128]{0:T(128)}) custom-call(bf16[4,32,1280]{2,1,0:T(8,128)(2,1)} %pe_in.1, f32[4,32,1280]{2,1,0:T(8,128)} %pert_in.1, bf16[4,32,1280]{2,1,0:T(8,128)(2,1)} %tgt_in.1, f32[1280]{0:T(1024)} %gain_in.1, f32[1280]{0:T(1024)} %bias_in.1, bf16[12,40,1280]{2,1,0:T(8,128)(2,1)} %bitcast.4, ...), custom_call_target="tpu_custom_call" | custom-call | tf_op jit(solution)/shard_map/pallas_call | solution.py:770
  90.4 0.0 copy-done
  90.5 2.1 %multiply_add_fusion = f32[4,32,1280]{2,1,0:T(8,128)} fusion(f32[4,32,1280]{2,1,0:T(8,128)} %get-tuple-element.10, f32[4,32,1280]{2,1,0:T(8,128)S(1)} %copy-done, f32[4]{0:T(128)} %bitcast.7, f32[4]{0:T(128)} %bitcast.6), kind=kLoop, calls=%fused_computation | loop fusion | flops 491520 | bytes 1966112 | tf_op jit(solution)/shard_map/add | solution.py:794
Async XLA Ops:
  0.0 90.4 %copy-start = (f32[4,32,1280]{2,1,0:T(8,128)S(1)}, f32[4,32,1280]{2,1,0:T(8,128)}, u32[]{:S(2)}) copy-start(f32[4,32,1280]{2,1,0:T(8,128)} %pert_in.1) | copy-start | bytes 1966084
